TPU v7x, 256 devices: a whole 4x4x8 slice. The times are simulated.
256 devices in a mesh: head: 16 (over y, x), batch: 16 (over z, core).
Axes of the slice: x: 4, y: 4, z: 8, core: 2. Of those that a mesh axis runs over, the one named last changes fastest.
Arguments:
- hidden_in: bfloat16 [16, 256, 4096], P('batch', None, 'head')
- w_query: bfloat16 [4096, 4096], P('batch', 'head'), may hold values from -0.09375 to 0.09375
- w_key: bfloat16 [4096, 4096], P('batch', 'head'), may hold values from -0.09375 to 0.09375
- w_value: bfloat16 [4096, 4096], P('batch', 'head'), may hold values from -0.09375 to 0.09375
- w_beta: bfloat16 [4096, 32], P('batch', 'head'), may hold values from -0.09375 to 0.09375
- w_out: bfloat16 [4096, 4096], P('head', 'batch'), may hold values from -0.125 to 0.125
- mem_pos: int32 [16, 2, 64], P('batch'), may hold values from 0 to 127, as said below
- memory_in: float32 [16, 32, 128, 128], P('batch', 'head'), may hold values from -6 to 6
Outputs:
- hidden_out: bfloat16 [16, 256, 4096], P('batch', None, 'head')
- memory_out: float32 [16, 32, 128, 128], P('batch', 'head')
Inputs may be any that keep to these rules, and one draw needn't show every extreme that they name: `mem_pos`: within each sequence and segment the 64 positions are distinct and ascending.
All inputs are finite; a program needn't handle non-finite values.
Results may differ from a plain program's by a relative error of at most 0.005.
Values may be sent and summed in bfloat16 or wider, within the bound.
A program may use at most 64 MiB of HBM per device.

v0:
```python
import jax
import jax.numpy as jnp
from jax import lax
from jax.sharding import Mesh
from jax.sharding import PartitionSpec as P

SEGS = 2
HEAD = ("head_0", "head_1")


epsilon = 1e-05


def laid_out(pieces, dim):
    shape = list(pieces.shape[1:])
    shape[dim] *= pieces.shape[0]
    return jnp.moveaxis(pieces, 0, dim).reshape(shape)


def from_everyone(shard, axis):
    copies = jnp.broadcast_to(shard, (lax.axis_size(axis), *shard.shape))
    return lax.all_to_all(copies, axis, split_axis=0, concat_axis=0, tiled=True)


def gathered_copies(shard, axis, dim):
    return laid_out(from_everyone(shard, axis), dim)


def side_by_side(arrays, axis, dim, along):
    ends, at = ([], 0)
    for a in arrays[:-1]:
        at += a.shape[along]
        ends.append(at)
    both = jnp.concatenate(arrays, axis=along)
    return tuple(jnp.split(lax.all_gather(both, axis, axis=dim, tiled=True), ends, axis=along))


def gather_axes(shard, axes, dim):
    for axis in reversed(axes):
        shard = lax.all_gather(shard, axis, axis=dim, tiled=True)
    return shard


def recur(query, keys, values, beta, state):
    highest = lax.Precision.HIGHEST
    readouts = []
    for segment in range(query.shape[1]):
        readouts.append(
            jnp.einsum("bhij,blhj->blhi", state, query[:, segment], precision=highest).astype(
                jnp.bfloat16
            )
        )
        recalled = jnp.einsum("bhij,bmhj->bmhi", state, keys[:, segment], precision=highest)
        change = beta[:, segment][..., None] * (values[:, segment] - recalled)
        state = state + jnp.einsum("bmhi,bmhj->bhij", change, keys[:, segment], precision=highest)
    return (jnp.stack(readouts, axis=1), state)


def body(hidden_in, w_query, w_key, w_value, w_beta, w_out, mem_pos, memory_in):
    seq_count, row_count, local_width = hidden_in.shape
    seg_rows = row_count // SEGS
    mem_count = mem_pos.shape[2]
    local_heads = w_beta.shape[1]
    local_features = w_query.shape[1]
    head_size = local_features // local_heads
    x_float = hidden_in.astype(jnp.float32)
    whole = gathered_copies(hidden_in, HEAD, 2)
    whole_float = whole.astype(jnp.float32)
    mean_square = jnp.mean(whole_float * whole_float, axis=2, keepdims=True)
    normed = (whole_float * lax.rsqrt(mean_square + epsilon)).astype(jnp.bfloat16)
    full_width = normed.shape[2]
    offsets = (jnp.arange(SEGS, dtype=jnp.int32) * seg_rows)[None, :, None]
    picked = (mem_pos + offsets).reshape(seq_count, SEGS * mem_count)
    memory_rows = jax.vmap(lambda block, where: jnp.take(block, where, axis=0))(normed, picked)
    memory_rows = memory_rows.reshape(seq_count * SEGS * mem_count, full_width)
    token_rows = normed.reshape(seq_count * row_count, full_width)
    piece_query, piece_key, piece_value, piece_beta = side_by_side(
        (w_query, w_key, w_value, w_beta), "batch", 0, 1
    )
    query = jnp.dot(token_rows, piece_query, preferred_element_type=jnp.float32)
    keys = jnp.dot(memory_rows, piece_key, preferred_element_type=jnp.float32)
    values = jnp.dot(memory_rows, piece_value, preferred_element_type=jnp.float32)
    logits = jnp.dot(memory_rows, piece_beta, preferred_element_type=jnp.float32)
    query = (query * head_size ** (-0.5)).reshape(seq_count, SEGS, seg_rows, local_heads, head_size)
    keys = keys.reshape(seq_count, SEGS, mem_count, local_heads, head_size)
    keys = keys * lax.rsqrt(jnp.sum(keys * keys, axis=-1, keepdims=True) + 1e-06)
    values = values.reshape(seq_count, SEGS, mem_count, local_heads, head_size)
    beta = jax.nn.sigmoid(logits).reshape(seq_count, SEGS, mem_count, local_heads)
    readout, state = recur(query, keys, values, beta, memory_in)
    readout = readout.reshape(seq_count * row_count, local_features)
    all_columns = gathered_copies(w_out, "batch", 1)
    stacked = lax.all_to_all(all_columns, HEAD, split_axis=1, concat_axis=0, tiled=True)
    every_head = gather_axes(readout, HEAD, 1)
    mixed = jnp.dot(every_head, stacked, preferred_element_type=jnp.float32)
    hidden_out = (mixed + x_float.reshape(seq_count * row_count, local_width)).astype(jnp.bfloat16)
    return (hidden_out.reshape(hidden_in.shape), state)


def solution(mesh):
    split = Mesh(mesh.devices.reshape(4, 4, mesh.shape["batch"]), ("head_0", "head_1", "batch"))
    return jax.shard_map(
        body,
        mesh=split,
        in_specs=(
            P("batch", None, HEAD),
            P("batch", HEAD),
            P("batch", HEAD),
            P("batch", HEAD),
            P("batch", HEAD),
            P(HEAD, "batch"),
            P("batch", None, None),
            P("batch", HEAD, None, None),
        ),
        out_specs=(P("batch", None, HEAD), P("batch", HEAD, None, None)),
        check_vma=False,
    )
```

profile of v0, /device:TPU:1, one launch (start us, length us, event | category | flops | bytes accessed | tf_op | source)
XLA Modules:
  0.0 175.1 jit_solution(2233241443110707387)
XLA Ops:
  7.2 0.0 all-gather.3.cloned.1.call-start
  7.2 0.8 copy.47
  8.0 1.9 %pad_maximum_fusion = bf16[256,770]{1,0:T(8,128)(2,1)} fusion(bf16[256,2]{1,0:T(8,128)(2,1)S(1)} %copy.47, bf16[256,256]{1,0:T(8,128)(2,1)} %param.11, bf16[256,256]{1,0:T(8,128)(2,1)} %param.10, bf16[256,256]{1,0:T(8,128)(2,1)} %param.9), kind=kLoop, calls=%fused_computation.38 | loop fusion | flops 1576960 | bytes 788480 | tf_op jit(solution)/shard_map/concatenate | solution.py:34
  9.9 0.0 all-gather.3.cloned.1.call-update
  9.9 2.5 %broadcast_in_dim.23 = bf16[16,1,256,256]{3,2,1,0:T(8,128)(2,1)} broadcast(bf16[256,256]{1,0:T(8,128)(2,1)} %bitcast.136), dimensions={2,3} | broadcast | bytes 2228224 | tf_op jit(solution)/shard_map/broadcast_in_dim | solution.py:21
  12.4 0.0 copy-start.7
  12.4 0.0 copy-start.5
  12.4 7.7 %all-to-all-start = ((bf16[16,1,256,256]{3,2,1,0:T(8,128)(2,1)}), bf16[16,1,256,256]{3,2,1,0:T(8,128)(2,1)S(1)}, u32[]{:S(2)}, u32[]{:S(2)}) async-start(bf16[16,1,256,256]{3,2,1,0:T(8,128)(2,1)} %broadcast_in_dim.23), calls=%async_computation | async-start | bytes 4194304 | tf_op jit(solution)/shard_map/all_to_all | solution.py:22
  20.2 0.0 copy-done.7
  20.2 0.1 broadcast_add_fusion
  20.3 0.1 reshape.311
  20.3 0.1 reshape.310
  20.5 30.7 %all-to-all-done = bf16[16,1,256,256]{3,2,1,0:T(8,128)(2,1)S(1)} async-done(((bf16[16,1,256,256]{3,2,1,0:T(8,128)(2,1)}), bf16[16,1,256,256]{3,2,1,0:T(8,128)(2,1)S(1)}, u32[]{:S(2)}, u32[]{:S(2)}) %all-to-all-start) | async-done | bytes 2097184 | tf_op jit(solution)/shard_map/all_to_all | solution.py:22
  51.1 0.0 copy-done.5
  51.1 0.0 copy-start.2
  51.1 1.8 %broadcast_in_dim.28 = bf16[16,256,256]{2,1,0:T(8,128)(2,1)} broadcast(bf16[256,256]{1,0:T(8,128)(2,1)S(1)} %copy-done.5), dimensions={1,2} | broadcast | bytes 2228224 | tf_op jit(solution)/shard_map/broadcast_in_dim | solution.py:21
  52.9 0.3 copy-done.2
  53.2 10.2 %all-to-all-start.1 = ((bf16[16,256,256]{2,1,0:T(8,128)(2,1)}), bf16[16,256,256]{2,1,0:T(8,128)(2,1)}, u32[]{:S(2)}, u32[]{:S(2)}) async-start(bf16[16,256,256]{2,1,0:T(8,128)(2,1)} %broadcast_in_dim.28), calls=%async_computation.1 | async-start | bytes 4194304 | tf_op jit(solution)/shard_map/all_to_all | solution.py:22
  63.5 0.0 all-gather.5.cloned.1.call-start
  63.5 2.9 %copy.46 = bf16[16,1,256,256]{2,3,0,1:T(8,128)(2,1)S(1)} copy(bf16[16,1,256,256]{3,2,1,0:T(8,128)(2,1)} %copy-done.2) | data formatting | bytes 4194304 | tf_op jit(solution)/shard_map/all_to_all | solution.py:22
  66.4 0.0 copy-start
  66.4 2.8 %convert_element_type.82 = f32[16,1,256,256]{2,3,0,1:T(8,128)} convert(bf16[16,1,256,256]{2,3,0,1:T(8,128)(2,1)S(1)} %copy.46) | non-fusion elementwise | flops 1048576 | bytes 6291456 | tf_op jit(solution)/shard_map/convert_element_type | solution.py:68
  69.1 5.7 %copy.58 = f32[1,256,4096]{2,1,0:T(8,128)} copy(f32[1,256,4096]{1,2,0:T(8,128)} %bitcast.130) | data formatting | bytes 8388608 | tf_op jit(solution)/shard_map/convert_element_type | solution.py:68
  74.9 0.0 copy-done
  74.9 0.6 multiply_reduce_fusion
  75.5 2.6 %multiply_convert_fusion = bf16[1,256,4096]{2,1,0:T(8,128)(2,1)S(1)} fusion(f32[1,256,4096]{2,1,0:T(8,128)} %copy.58, f32[256]{0:T(256)S(1)} %add_rsqrt_fusion.1), kind=kLoop, calls=%fused_computation.3 | loop fusion | flops 2097152 | bytes 6292480 | tf_op jit(solution)/shard_map/convert_element_type | solution.py:70
  78.1 4.7 %gather_fusion = bf16[128,4096]{1,0:T(8,128)(2,1)} fusion(bf16[1,256,4096]{2,1,0:T(8,128)(2,1)S(1)} %multiply_convert_fusion, s32[128]{0:T(128)S(1)} %or_bitcast_fusion), kind=kCustom, calls=%fused_computation | custom fusion | bytes 2098176 | tf_op jit(solution)/shard_map/vmap(jit(_take))/gather | solution.py:74
  82.9 0.0 copy-start.1
  82.9 1.5 bitcast_select_fusion
  84.4 0.4 copy-done.1
  84.8 0.0 copy-start.3
  84.8 1.9 %fusion = bf16[256,4096]{0,1:T(8,128)(2,1)} fusion(f32[256]{0:T(256)S(1)} %add_rsqrt_fusion.1, bf16[16,1,256,256]{2,3,0,1:T(8,128)(2,1)S(1)} %copy-done.1), kind=kLoop, calls=%fused_computation.2 | loop fusion | flops 3145728 | bytes 4195328 | tf_op jit(solution)/shard_map/convert_element_type | solution.py:70
  86.6 0.0 copy-done.3
  86.7 2.1 %fusion.1 = f32[128,256]{1,0:T(8,128)S(1)} fusion(bf16[4096,770]{1,0:T(8,128)(2,1)} %all-gather.3.cloned.1.call-done, bf16[128,4096]{1,0:T(8,128)(2,1)S(1)} %copy-done.3, pred[128]{0:T(512)(128)(4,1)S(1)} %compare_and_fusion), kind=kOutput, calls=%fused_computation.5 | convolution fusion | flops 268959744 | bytes 3276928 | tf_op jit(solution)/shard_map/dot_general | solution.py:81
  88.7 0.1 reshape.313
  88.8 3.0 %slice_bitcast_fusion = bf16[256,4096]{0,1:T(8,128)(2,1)} fusion(bf16[4096,770]{1,0:T(8,128)(2,1)} %all-gather.3.cloned.1.call-done), kind=kLoop, calls=%fused_computation.7 | loop fusion | bytes 4194304 | tf_op jit(solution)/shard_map/dot_general | solution.py:82
  91.9 0.2 multiply_reduce_fusion.1
  92.1 0.1 copy.53
  92.2 2.9 %copy.52 = bf16[256,4096]{1,0:T(8,128)(2,1)S(1)} copy(bf16[256,4096]{0,1:T(8,128)(2,1)} %slice_bitcast_fusion) | data formatting | bytes 4194304 | tf_op jit(solution)/shard_map/dot_general | solution.py:82
  95.1 2.0 %fusion.22 = f32[128,2]{0,1:T(2,128)S(1)} fusion(bf16[4096,770]{1,0:T(8,128)(2,1)} %all-gather.3.cloned.1.call-done, bf16[128,4096]{1,0:T(8,128)(2,1)} %gather_fusion, pred[128]{0:T(512)(128)(4,1)S(1)} %compare_and_fusion), kind=kOutput, calls=%fused_computation.34 | convolution fusion | flops 2622208 | bytes 2098304 | tf_op jit(solution)/shard_map/dot_general | solution.py:83
  97.1 0.1 reshape.312
  97.2 0.0 copy-start.4
  97.2 3.8 %fusion.5 = f32[256,256]{1,0:T(8,128)} fusion(bf16[256,4096]{0,1:T(8,128)(2,1)} %fusion, bf16[4096,770]{1,0:T(8,128)(2,1)} %all-gather.3.cloned.1.call-done), kind=kOutput, calls=%fused_computation.10 | convolution fusion | flops 536936448 | bytes 4456448 | tf_op jit(solution)/shard_map/dot_general | solution.py:80
  101.0 1.8 %reshape.306 = f32[1,2,128,2,128]{4,3,2,1,0:T(2,128)} reshape(f32[256,256]{1,0:T(8,128)} %fusion.5) | data formatting | bytes 524288 | tf_op jit(solution)/shard_map/reshape | solution.py:84
  102.7 1.0 fusion.30
  103.7 0.0 copy-done.4
  103.7 0.4 fusion.12
  104.2 0.1 copy_multiply_fusion
  104.3 0.8 convolution_bitcast_fusion.2
  105.1 0.4 fusion.19
  105.5 0.4 fusion.10
  105.9 0.4 fusion.13
  106.3 0.1 copy.55
  106.5 11.0 %all_gather.10 = bf16[256,1024]{1,0:T(8,128)(2,1)} all-gather(bf16[256,256]{1,0:T(8,128)(2,1)S(1)} %bitcast.134), channel_id=1, replica_groups=mesh['head_0'=4,'head_1'=4,'batch'=16] {'head_1'}, dimensions={1}, use_global_device_ids=true | all-gather | bytes 655360 | tf_op jit(solution)/shard_map/all_gather | solution.py:40
  117.5 0.0 all-gather.5.cloned.1.call-update
  117.5 0.0 all-to-all-done.1
  117.5 0.0 copy-start.6
  117.5 3.9 %all-to-all-start.2 = ((bf16[256,16,256]{2,0,1:T(8,128)(2,1)}), bf16[256,16,256]{2,0,1:T(8,128)(2,1)S(1)}, u32[]{:S(2)}, u32[]{:S(2)}) async-start(bf16[256,16,256]{2,0,1:T(8,128)(2,1)} %bitcast.31), calls=%async_computation.2 | async-start | bytes 4194304 | tf_op jit(solution)/shard_map/all_to_all | solution.py:92
  121.4 0.4 fusion.16
  121.8 1.0 fusion.11
  122.8 23.4 %all-to-all-done.2 = bf16[256,16,256]{2,0,1:T(8,128)(2,1)S(1)} async-done(((bf16[256,16,256]{2,0,1:T(8,128)(2,1)}), bf16[256,16,256]{2,0,1:T(8,128)(2,1)S(1)}, u32[]{:S(2)}, u32[]{:S(2)}) %all-to-all-start.2) | async-done | bytes 2097184 | tf_op jit(solution)/shard_map/all_to_all | solution.py:92
  146.3 19.0 %all-gather.5.cloned.1.call-done = bf16[256,4096]{1,0:T(8,128)(2,1)} async-done(((bf16[256,1024]{1,0:T(8,128)(2,1)}), bf16[256,4096]{1,0:T(8,128)(2,1)}) %all-gather.5.cloned.1.call-update) | async-done | bytes 2097168 | tf_op jit(solution)/shard_map/all_gather | solution.py:40
  165.3 0.0 copy-done.6
  165.3 3.0 %fusion.9 = bf16[1,256,256]{2,1,0:T(8,128)(2,1)} fusion(bf16[256,4096]{1,0:T(8,128)(2,1)} %all-gather.5.cloned.1.call-done, bf16[4096,256]{1,0:T(8,128)(2,1)S(1)} %bitcast.133, bf16[1,256,256]{2,1,0:T(8,128)(2,1)S(1)} %copy-done.6), kind=kOutput, calls=%fused_computation.13 | convolution fusion | flops 537067520 | bytes 4456448 | tf_op jit(solution)/shard_map/dot_general | solution.py:94
  (11 shorter events, 0.1 us)
Async XLA Ops:
  7.2 79.5 %all-gather.3.cloned.1.call-start = ((), (), s32[]{:S(2)}) async-start(), calls=%async_computation.3 | async-start | bytes 7798784 | tf_op jit(solution)/shard_map/all_gather | solution.py:35
  12.4 7.7 %copy-start.7 = (s32[1,2,64]{2,1,0:T(2,128)S(1)}, s32[1,2,64]{2,1,0:T(2,128)}, u32[]{:S(2)}) copy-start(s32[1,2,64]{2,1,0:T(2,128)} %param.14) | copy-start | bytes 1540
  12.4 38.7 %copy-start.5 = (bf16[256,256]{1,0:T(8,128)(2,1)S(1)}, bf16[256,256]{1,0:T(8,128)(2,1)}, u32[]{:S(2)}) copy-start(bf16[256,256]{1,0:T(8,128)(2,1)} %param.13) | copy-start | bytes 393220
  12.4 38.7 %all-to-all-start = ((bf16[16,1,256,256]{3,2,1,0:T(8,128)(2,1)}), bf16[16,1,256,256]{3,2,1,0:T(8,128)(2,1)S(1)}, u32[]{:S(2)}, u32[]{:S(2)}) async-start(bf16[16,1,256,256]{3,2,1,0:T(8,128)(2,1)} %broadcast_in_dim.23), calls=%async_computation | async-start | bytes 4194304 | tf_op jit(solution)/shard_map/all_to_all | solution.py:22
  51.1 2.1 %copy-start.2 = (bf16[16,1,256,256]{3,2,1,0:T(8,128)(2,1)}, bf16[16,1,256,256]{3,2,1,0:T(8,128)(2,1)S(1)}, u32[]{:S(2)}) copy-start(bf16[16,1,256,256]{3,2,1,0:T(8,128)(2,1)S(1)} %all-to-all-done) | copy-start | bytes 6291460
  53.2 64.3 %all-to-all-start.1 = ((bf16[16,256,256]{2,1,0:T(8,128)(2,1)}), bf16[16,256,256]{2,1,0:T(8,128)(2,1)}, u32[]{:S(2)}, u32[]{:S(2)}) async-start(bf16[16,256,256]{2,1,0:T(8,128)(2,1)} %broadcast_in_dim.28), calls=%async_computation.1 | async-start | bytes 4194304 | tf_op jit(solution)/shard_map/all_to_all | solution.py:22
  63.5 101.8 %all-gather.5.cloned.1.call-start = ((), (), s32[]{:S(2)}) async-start(), calls=%async_computation.4 | async-start | bytes 2621440 | tf_op jit(solution)/shard_map/all_gather | solution.py:40
  66.4 8.5 %copy-start = (bf16[16,1,256,256]{2,3,0,1:T(8,128)(2,1)}, bf16[16,1,256,256]{2,3,0,1:T(8,128)(2,1)S(1)}, u32[]{:S(2)}) copy-start(bf16[16,1,256,256]{2,3,0,1:T(8,128)(2,1)S(1)} %copy.46) | copy-start | bytes 6291460
  82.9 1.9 %copy-start.1 = (bf16[16,1,256,256]{2,3,0,1:T(8,128)(2,1)S(1)}, bf16[16,1,256,256]{2,3,0,1:T(8,128)(2,1)}, u32[]{:S(2)}) copy-start(bf16[16,1,256,256]{2,3,0,1:T(8,128)(2,1)} %copy-done) | copy-start | bytes 6291460
  84.8 1.9 %copy-start.3 = (bf16[128,4096]{1,0:T(8,128)(2,1)S(1)}, bf16[128,4096]{1,0:T(8,128)(2,1)}, u32[]{:S(2)}) copy-start(bf16[128,4096]{1,0:T(8,128)(2,1)} %gather_fusion) | copy-start | bytes 3145732
  97.2 6.6 %copy-start.4 = (f32[1,2,128,128]{3,2,1,0:T(8,128)S(1)}, f32[1,2,128,128]{3,2,1,0:T(8,128)}, u32[]{:S(2)}) copy-start(f32[1,2,128,128]{3,2,1,0:T(8,128)} %param.15) | copy-start | bytes 393220
  117.5 47.7 %copy-start.6 = (bf16[1,256,256]{2,1,0:T(8,128)(2,1)S(1)}, bf16[1,256,256]{2,1,0:T(8,128)(2,1)}, u32[]{:S(2)}) copy-start(bf16[1,256,256]{2,1,0:T(8,128)(2,1)} %param.8) | copy-start | bytes 393220
  117.5 28.7 %all-to-all-start.2 = ((bf16[256,16,256]{2,0,1:T(8,128)(2,1)}), bf16[256,16,256]{2,0,1:T(8,128)(2,1)S(1)}, u32[]{:S(2)}, u32[]{:S(2)}) async-start(bf16[256,16,256]{2,0,1:T(8,128)(2,1)} %bitcast.31), calls=%async_computation.2 | async-start | bytes 4194304 | tf_op jit(solution)/shard_map/all_to_all | solution.py:92
Sparse Core Ops, SparseCore 0:
  10.1 55.0 all-gather.2
  117.6 47.5 all-gather.4
where the time goes:
time: 176 us; the launch traced here: 175 us
  waiting for transfers between devices  73.1 us (42%)
  local copies, waits for them, and re-layouts  28.4 us (16%)
  starting transfers between devices  21.9 us (12%)
  matrix products  14.6 us (8%)
  between operations  14.3 us (8%)
  other arithmetic  11.7 us (7%)
  blocking collectives  11 us (6%)
    all_to_all x2, waiting for transfers between devices, from_everyone(): return lax.all_to_all(copies, axis, split_axis=0, concat_axis=0, tiled=True)  30.7 us
    all_to_all x1, waiting for transfers between devices, body(): lax.all_to_all(all_columns, HEAD, split_axis=1, concat_axis=0, tiled=True)  23.4 us
    all_gather x1, waiting for transfers between devices, gather_axes(): shard = lax.all_gather(shard, axis, axis=dim, tiled=True)  19 us
    all_to_all x2, starting transfers between devices, from_everyone(): return lax.all_to_all(copies, axis, split_axis=0, concat_axis=0, tiled=True)  18 us
    all_gather x1, blocking collectives, gather_axes(): shard = lax.all_gather(shard, axis, axis=dim, tiled=True)  11 us
    dot_general x2, local copies, waits for them, and re-layouts, body(): jnp.dot(memory_rows, piece_value, preferred_element_type=jnp.float32)  5.96 us
    convert_element_type x1, local copies, waits for them, and re-layouts, body(): whole_float = whole.astype(jnp.float32)  5.73 us
    gather x2, local copies, waits for them, and re-layouts, body(): jnp.take(block, where, axis=0)  4.76 us
  transfers between devices with their start and end apart: 5, of which 3 were waited for; matrix products, arithmetic and copies ran while one was open for 28% of the time, Pallas kernels for 0%

commit v1 on v0

v1 whole, which is shorter than its diff:
```python
import jax
import jax.numpy as jnp
from jax import lax
from jax.experimental import pallas as pl
from jax.experimental.pallas import tpu as pltpu
from jax.sharding import Mesh
from jax.sharding import PartitionSpec as P

HEAD = ("y", "x")
BATCH = ("z", "c")
EPS = 1e-05
F32 = jnp.float32
BF16 = jnp.bfloat16
HIGHEST = lax.Precision.HIGHEST
NN = (((1,), (0,)), ((), ()))
NT = (((1,), (1,)), ((), ()))
TN = (((0,), (0,)), ((), ()))


def dot(a, b, dims=NN, precision=None):
    return lax.dot_general(a, b, dims, precision=precision, preferred_element_type=F32)


class Copies:
    def __init__(self, send, recv):
        self.send, self.recv, self.count, self.sent = send, recv, 0, []

    def post(self, src, dst, to, recv=None):
        slot = self.count
        self.count += 1
        copy = pltpu.make_async_remote_copy(
            src_ref=src,
            dst_ref=dst,
            send_sem=self.send.at[slot],
            recv_sem=self.recv.at[slot],
            device_id=to,
            device_id_type=pl.DeviceIdType.MESH,
        )
        copy.start()
        self.sent.append(copy)
        return slot

    def arrived(self, slot, ref):
        pltpu.make_async_copy(ref, ref, self.recv.at[slot]).wait()

    def drain(self):
        for copy in self.sent:
            copy.wait_send()


def kernel(
    x_in, wq_in, wk_in, wv_in, wb_in, wo_in, pos_in, mem_in,
    out_ref, memory_ref,
    xg, xn, xm, gv, gq, gk, go, parts, wb_v, pos_v, state,
    acc_q, acc_k, acc_v, logits, readout,
    half_a, half_b, full_a, full_b, sum_a, sum_b, half2_a, half2_b, full2_a, full2_b,
    local, send, recv,
):
    y, x, z, c = (lax.axis_index(n) for n in ("y", "x", "z", "c"))
    ny = lambda d: lax.rem(y + (d % 4), 4)
    nx = lambda d: lax.rem(x + (d % 4), 4)
    nz = lambda d: lax.rem(z + (d % 8), 8)
    up, down = {"z": nz(1)}, {"z": nz(-1)}
    xp, xd = {"x": nx(1)}, {"x": nx(-1)}
    yp, yd = {"y": ny(1)}, {"y": ny(-1)}
    partner = {"c": 1 - c}
    mine = z * 2 + c

    barrier = pltpu.get_barrier_semaphore()
    for peer in (up, down, xp, xd, yp, yd, partner):
        pl.semaphore_signal(barrier, inc=1, device_id=peer, device_id_type=pl.DeviceIdType.MESH)

    loads = [
        (wb_in, wb_v),
        (wv_in, gv.at[mine]),
        (wq_in, gq.at[mine]),
        (x_in.at[0], xg.at[y, x]),
        (wk_in, gk.at[mine, 0:256]),
        (wo_in, go.at[mine]),
        (pos_in.at[0], pos_v),
        (mem_in.at[0], state),
    ]
    fetched = []
    for i, (src, dst) in enumerate(loads):
        copy = pltpu.make_async_copy(src, dst, local.at[i])
        copy.start()
        fetched.append(copy)

    fetched[0].wait()
    rows = jnp.concatenate([wb_v[...].astype(F32), jnp.zeros((14, 256), F32)], axis=0)
    gk[mine, 256:272, :] = rows.astype(BF16)
    for copy in fetched[1:]:
        copy.wait()

    pl.semaphore_wait(barrier, 7)
    net = Copies(send, recv)

    def pass_on(buf, block, to):
        return net.post(buf.at[block], buf.at[block], to)

    main = (gv, gq, gk)
    from_down, from_up, from_partner = {}, {}, {}

    def send_own(buf, m):
        from_down[m] = pass_on(buf, mine, up)
        from_up[m] = pass_on(buf, mine, down)

    def give_partner(buf, d, m):
        block = nz(d) * 2 + c
        from_partner[m, d] = pass_on(buf, block, partner)

    for m, buf in enumerate(main):
        send_own(buf, m)
    for m, buf in enumerate(main):
        give_partner(buf, 0, m)

    a0, a1, b0, b1 = slice(0, 64), slice(64, 128), slice(128, 192), slice(192, 256)
    top, low = slice(0, 128), slice(128, 256)

    def same(ref, to):
        return net.post(ref, ref, to)

    own_a, own_b = xg.at[y, x, top], xg.at[y, x, low]
    s = [same(own_a, xp), same(own_a, xd), same(own_b, yp), same(own_b, yd)]
    net.arrived(s[0], xg.at[y, nx(-1), top])
    f0 = same(xg.at[y, nx(-1), a0], xp)
    net.arrived(s[1], xg.at[y, nx(1), top])
    f1 = same(xg.at[y, nx(1), a1], xd)
    net.arrived(s[2], xg.at[ny(-1), x, low])
    f2 = same(xg.at[ny(-1), x, b0], yp)
    net.arrived(s[3], xg.at[ny(1), x, low])
    f3 = same(xg.at[ny(1), x, b1], yd)
    net.arrived(f0, xg.at[y, nx(2), a0])
    net.arrived(f1, xg.at[y, nx(2), a1])
    rows_a = lambda yy, r: xg.at[yy, :, r]
    s0 = same(rows_a(y, top), yp)
    s1 = same(rows_a(y, top), yd)
    net.arrived(f2, xg.at[ny(2), x, b0])
    net.arrived(f3, xg.at[ny(2), x, b1])
    rows_b = lambda xx, r: xg.at[:, xx, r]
    s2 = same(rows_b(x, low), xp)
    s3 = same(rows_b(x, low), xd)

    def relay(buf, m, d):
        net.arrived(from_down[m], buf.at[nz(-d) * 2 + c])
        ahead = pass_on(buf, nz(-d) * 2 + c, up)
        net.arrived(from_up[m], buf.at[nz(d) * 2 + c])
        behind = pass_on(buf, nz(d) * 2 + c, down)
        give_partner(buf, -d, m)
        give_partner(buf, d, m)
        from_down[m], from_up[m] = ahead, behind

    def relay_half(buf, m):
        lo, hi = nz(-3) * 2 + c, nz(3) * 2 + c
        net.arrived(from_down[m], buf.at[lo])
        part = buf.at[lo, 0:128]
        ahead = net.post(part, part, up)
        net.arrived(from_up[m], buf.at[hi])
        part = buf.at[hi, 128:]
        behind = net.post(part, part, down)
        give_partner(buf, -3, m)
        give_partner(buf, 3, m)
        from_down[m], from_up[m] = ahead, behind

    def far(buf, m):
        block = nz(4) * 2 + c
        net.arrived(from_down[m], buf.at[block, 0:128])
        net.arrived(from_up[m], buf.at[block, 128:])
        give_partner(buf, 4, m)

    def take(buf, m, d):
        net.arrived(from_partner[m, d], buf.at[nz(d) * 2 + (1 - c)])

    for m, buf in enumerate(main):
        relay(buf, m, 1)

    net.arrived(s0, rows_a(ny(-1), top))
    f0 = same(rows_a(ny(-1), a0), yp)
    net.arrived(s1, rows_a(ny(1), top))
    f1 = same(rows_a(ny(1), a1), yd)
    net.arrived(s2, rows_b(nx(-1), low))
    f2 = same(rows_b(nx(-1), b0), xp)
    net.arrived(s3, rows_b(nx(1), low))
    f3 = same(rows_b(nx(1), b1), xd)
    net.arrived(f0, rows_a(ny(2), a0))
    net.arrived(f1, rows_a(ny(2), a1))
    net.arrived(f2, rows_b(nx(2), b0))
    net.arrived(f3, rows_b(nx(2), b1))

    def squares(i, total):
        v = xg[i // 4, lax.rem(i, 4)].astype(F32)
        return total + v * v

    total = lax.fori_loop(0, 16, squares, jnp.zeros((256, 256), F32))
    scale = lax.rsqrt(jnp.sum(total, axis=1, keepdims=True) * (1.0 / 4096) + EPS)
    row = lax.broadcasted_iota(jnp.int32, (256, 128), 0)
    where = jnp.concatenate([pos_v[0:1, :], pos_v[1:2, :] + 128], axis=1)
    chosen = jnp.where(row == where, 1.0, 0.0).T.astype(BF16)

    def normalise(i, carry):
        v = xg[i // 4, lax.rem(i, 4)].astype(F32)
        n = (v * scale).astype(BF16)
        xn[i] = n
        xm[i] = dot(chosen, n).astype(BF16)
        return carry

    lax.fori_loop(0, 16, normalise, 0)

    acc_q[...] = jnp.zeros_like(acc_q)
    acc_k[...] = jnp.zeros_like(acc_k)
    acc_v[...] = jnp.zeros_like(acc_v)
    logits[...] = jnp.zeros_like(logits)

    def project(block):
        rows = xm[block]
        acc_v[...] += dot(rows, gv[block])
        acc_q[...] += dot(xn[block], gq[block])
        acc_k[...] += dot(rows, gk[block, 0:256])
        logits[...] += dot(rows, gk[block, 256:272], NT)

    def project_pair(d):
        for m, buf in enumerate(main):
            take(buf, m, d)
        project(nz(d) * 2)
        project(nz(d) * 2 + 1)

    project_pair(0)
    for m, buf in enumerate(main):
        relay(buf, m, 2)
    send_own(go, 3)
    give_partner(go, 0, 3)
    project_pair(-1)
    project_pair(1)
    for m, buf in enumerate(main):
        relay_half(buf, m)
    project_pair(-2)
    project_pair(2)
    relay(go, 3, 1)
    for m, buf in enumerate(main):
        far(buf, m)
    project_pair(-3)
    project_pair(3)
    relay(go, 3, 2)
    project_pair(4)

    for h in range(2):
        cols = slice(h * 128, h * 128 + 128)
        q = acc_q[:, cols] * (128.0 ** -0.5)
        k = acc_k[:, cols]
        k = k * lax.rsqrt(jnp.sum(k * k, axis=1, keepdims=True) + 1e-06)
        v = acc_v[:, cols]
        beta = jax.nn.sigmoid(logits[:, h:h + 1])
        st = state[h]
        for seg in range(2):
            m = slice(seg * 64, seg * 64 + 64)
            t = slice(seg * 128, seg * 128 + 128)
            readout[t, cols] = dot(q[t], st, NT, HIGHEST).astype(BF16)
            change = beta[m] * (v[m] - dot(k[m], st, NT, HIGHEST))
            st = st + dot(change, k[m], TN, HIGHEST)
        memory_ref[0, h] = st

    relay_half(go, 3)
    far(go, 3)
    for d in (0, -1, 1, -2, 2, -3, 3, 4):
        take(go, 3, d)

    def partial(i, carry):
        parts[i // 4, lax.rem(i, 4)] = dot(readout[...], go[i]).astype(BF16)
        return carry

    lax.fori_loop(0, 16, partial, 0)

    h0 = net.post(parts.at[:, nx(2), a0], half_a.at[0], xp)
    h1 = net.post(parts.at[:, nx(2), a1], half_a.at[1], xd)
    h2 = net.post(parts.at[ny(2), :, b0], half_b.at[0], yp)
    h3 = net.post(parts.at[ny(2), :, b1], half_b.at[1], yd)

    def add(dst, src):
        dst[...] = (dst[...].astype(F32) + src[...].astype(F32)).astype(BF16)

    net.arrived(h0, half_a.at[0])
    add(parts.at[:, nx(1), a0], half_a.at[0])
    h0 = net.post(parts.at[:, nx(1), top], full_a.at[0], xp)
    net.arrived(h1, half_a.at[1])
    add(parts.at[:, nx(-1), a1], half_a.at[1])
    h1 = net.post(parts.at[:, nx(-1), top], full_a.at[1], xd)
    net.arrived(h2, half_b.at[0])
    add(parts.at[ny(1), :, b0], half_b.at[0])
    h2 = net.post(parts.at[ny(1), :, low], full_b.at[0], yp)
    net.arrived(h3, half_b.at[1])
    add(parts.at[ny(-1), :, b1], half_b.at[1])
    h3 = net.post(parts.at[ny(-1), :, low], full_b.at[1], yd)

    net.arrived(h0, full_a.at[0])
    net.arrived(h1, full_a.at[1])
    sum_a[...] = (
        parts[:, x, top].astype(F32) + full_a[0].astype(F32) + full_a[1].astype(F32)
    ).astype(BF16)
    g0 = net.post(sum_a.at[ny(2), a0], half2_a.at[0], yp)
    g1 = net.post(sum_a.at[ny(2), a1], half2_a.at[1], yd)
    net.arrived(h2, full_b.at[0])
    net.arrived(h3, full_b.at[1])
    sum_b[...] = (
        parts[y, :, low].astype(F32) + full_b[0].astype(F32) + full_b[1].astype(F32)
    ).astype(BF16)
    g2 = net.post(sum_b.at[nx(2), a0], half2_b.at[0], xp)
    g3 = net.post(sum_b.at[nx(2), a1], half2_b.at[1], xd)

    net.arrived(g0, half2_a.at[0])
    add(sum_a.at[ny(1), a0], half2_a.at[0])
    g0 = net.post(sum_a.at[ny(1)], full2_a.at[0], yp)
    net.arrived(g1, half2_a.at[1])
    add(sum_a.at[ny(-1), a1], half2_a.at[1])
    g1 = net.post(sum_a.at[ny(-1)], full2_a.at[1], yd)
    net.arrived(g2, half2_b.at[0])
    add(sum_b.at[nx(1), a0], half2_b.at[0])
    g2 = net.post(sum_b.at[nx(1)], full2_b.at[0], xp)
    net.arrived(g3, half2_b.at[1])
    add(sum_b.at[nx(-1), a1], half2_b.at[1])
    g3 = net.post(sum_b.at[nx(-1)], full2_b.at[1], xd)

    net.arrived(g0, full2_a.at[0])
    net.arrived(g1, full2_a.at[1])
    mixed = sum_a[y].astype(F32) + full2_a[0].astype(F32) + full2_a[1].astype(F32)
    out_ref[0, top] = (xg[y, x, top].astype(F32) + mixed).astype(BF16)
    net.arrived(g2, full2_b.at[0])
    net.arrived(g3, full2_b.at[1])
    mixed = sum_b[x].astype(F32) + full2_b[0].astype(F32) + full2_b[1].astype(F32)
    out_ref[0, low] = (xg[y, x, low].astype(F32) + mixed).astype(BF16)
    net.drain()


COPIES = 144


def body(hidden_in, w_query, w_key, w_value, w_beta, w_out, mem_pos, memory_in):
    vmem = pltpu.VMEM
    scratch = [
        vmem((4, 4, 256, 256), BF16),
        vmem((16, 256, 256), BF16),
        vmem((16, 128, 256), BF16),
        vmem((16, 256, 256), BF16),
        vmem((16, 256, 256), BF16),
        vmem((16, 272, 256), BF16),
        vmem((16, 256, 256), BF16),
        vmem((4, 4, 256, 256), BF16),
        vmem((2, 256), BF16),
        vmem((2, 64), jnp.int32),
        vmem((2, 128, 128), F32),
        vmem((256, 256), F32),
        vmem((128, 256), F32),
        vmem((128, 256), F32),
        vmem((128, 16), F32),
        vmem((256, 256), BF16),
        vmem((2, 4, 64, 256), BF16),
        vmem((2, 4, 64, 256), BF16),
        vmem((2, 4, 128, 256), BF16),
        vmem((2, 4, 128, 256), BF16),
        vmem((4, 128, 256), BF16),
        vmem((4, 128, 256), BF16),
        vmem((2, 64, 256), BF16),
        vmem((2, 64, 256), BF16),
        vmem((2, 128, 256), BF16),
        vmem((2, 128, 256), BF16),
        pltpu.SemaphoreType.DMA((8,)),
        pltpu.SemaphoreType.DMA((COPIES,)),
        pltpu.SemaphoreType.DMA((COPIES,)),
    ]
    return pl.pallas_call(
        kernel,
        out_shape=(
            jax.ShapeDtypeStruct(hidden_in.shape, BF16),
            jax.ShapeDtypeStruct(memory_in.shape, F32),
        ),
        in_specs=[pl.BlockSpec(memory_space=pltpu.HBM)] * 8,
        out_specs=[pl.BlockSpec(memory_space=vmem)] * 2,
        scratch_shapes=scratch,
        compiler_params=pltpu.CompilerParams(
            collective_id=0, has_side_effects=True
        ),
    )(hidden_in, w_query, w_key, w_value, w_beta.T, w_out, mem_pos, memory_in)


def solution(mesh):
    split = Mesh(mesh.devices.reshape(4, 4, 8, 2), ("y", "x", "z", "c"))
    return jax.shard_map(
        body,
        mesh=split,
        in_specs=(
            P(BATCH, None, HEAD),
            P(BATCH, HEAD),
            P(BATCH, HEAD),
            P(BATCH, HEAD),
            P(BATCH, HEAD),
            P(HEAD, BATCH),
            P(BATCH, None, None),
            P(BATCH, HEAD, None, None),
        ),
        out_specs=(P(BATCH, None, HEAD), P(BATCH, HEAD, None, None)),
        check_vma=False,
    )
```

time: 176 us -> 89 us (0.51)
  Pallas kernels: 0 us -> 85.9 us
  waiting for transfers between devices: 73.1 us -> 0 us
  local copies, waits for them, and re-layouts: 28.4 us -> 2.26 us
  starting transfers between devices: 21.9 us -> 0 us
  matrix products: 14.6 us -> 0 us
  between operations: 14.3 us -> 0.65 us
  other arithmetic: 11.7 us -> 0 us
  blocking collectives: 11 us -> 0 us
    pallas_call x0 -> x1, Pallas kernels: none -> 85.9 us  [body(): pl.pallas_call(kernel, out_shape=(jax.ShapeDtypeStruct(hidden_in.shape, B...]
    all_to_all x3 -> x0, waiting for transfers between devices: 54.1 us -> none  [the longest x2 30.7 us: from_everyone(): return lax.all_to_all(copies, axis, split_axis=0, concat_axis=0, tiled=True)]
    all_to_all x3 -> x0, starting transfers between devices: 21.8 us -> none  [the longest x2 18 us: from_everyone(): return lax.all_to_all(copies, axis, split_axis=0, concat_axis=0, tiled=True)]
    all_gather x2 -> x0, waiting for transfers between devices: 19 us -> none  [the longest x1 19 us: gather_axes(): shard = lax.all_gather(shard, axis, axis=dim, tiled=True)]
    dot_general x11 -> x0, matrix products: 14.6 us -> none  [the longest x1 3.79 us: body(): query = jnp.dot(token_rows, piece_query, preferred_element_type=jnp.float32)]
    all_gather x1 -> x0, blocking collectives: 11 us -> none  [gather_axes(): shard = lax.all_gather(shard, axis, axis=dim, tiled=True)]
    convert_element_type x3 -> x0, other arithmetic: 7.29 us -> none  [the longest x2 4.53 us: body(): (whole_float * lax.rsqrt(mean_square + epsilon)).astype(jnp.bfloat16)]
    dot_general x2 -> x0, local copies, waits for them, and re-layouts: 5.96 us -> none  [body(): jnp.dot(memory_rows, piece_value, preferred_element_type=jnp.float32)]
  transfers between devices with their start and end apart: 5 -> 0, of which waited for: 3 -> 0; matrix products, arithmetic and copies ran while one was open for 28% -> 0% of each run, Pallas kernels for 0% -> 0%
where the time goes in v1:
time: 89 us; the launch traced here: 88.8 us
  Pallas kernels  85.9 us (97%)
  local copies, waits for them, and re-layouts  2.26 us (3%)
    pallas_call x1, Pallas kernels, body(): pl.pallas_call(kernel, out_shape=(jax.ShapeDtypeStruct(hidden_in.shape, B...  85.9 us
    unnamed x4, local copies, waits for them, and re-layouts  2.26 us

profile of v1, /device:TPU:1, one launch (start us, length us, event | category | flops | bytes accessed | tf_op | source)
XLA Modules:
  0.0 88.8 jit_solution(12979463866635229123)
XLA Ops:
  0.6 85.9 %shard_map.95 = (bf16[1,256,256]{2,1,0:T(8,128)(2,1)}, f32[1,2,128,128]{3,2,1,0:T(8,128)}) custom-call(bf16[1,256,256]{2,1,0:T(8,128)(2,1)} %x_in.1, bf16[256,256]{1,0:T(8,128)(2,1)} %wq_in.1, bf16[256,256]{1,0:T(8,128)(2,1)} %wk_in.1, bf16[256,256]{1,0:T(8,128)(2,1)} %wv_in.1, bf16[2,256]{1,0:T(2,128)(2,1)} %bitcast.1, bf16[256,256]{1,0:T(8,128)(2,1)} %wo_in.1, ...), custom_call_target="tpu_custom_call" | custom-call | tf_op jit(solution)/shard_map/pallas_call | solution.py:369
  86.5 0.0 copy-start
  86.5 1.6 %copy.12 = bf16[1,256,256]{2,1,0:T(8,128)(2,1)} copy(bf16[1,256,256]{2,1,0:T(8,128)(2,1)} %get-tuple-element.4) | data formatting | bytes 262144
  88.1 0.0 copy-done
  88.1 0.7 copy.13
Async XLA Ops:
  86.5 1.6 %copy-start = (f32[1,2,128,128]{3,2,1,0:T(8,128)S(1)}, f32[1,2,128,128]{3,2,1,0:T(8,128)}, u32[]{:S(2)}) copy-start(f32[1,2,128,128]{3,2,1,0:T(8,128)} %get-tuple-element.5) | copy-start | bytes 393220

commit v2 on v1

v2 whole, which is shorter than its diff:
```python
import functools

import jax
import jax.numpy as jnp
from jax import lax
from jax.experimental import pallas as pl
from jax.experimental.pallas import tpu as pltpu
from jax.sharding import Mesh
from jax.sharding import PartitionSpec as P

HEAD = ("y", "x")
BATCH = ("z", "c")
EPS = 1e-05
F32 = jnp.float32
BF16 = jnp.bfloat16
HIGHEST = lax.Precision.HIGHEST
NN = (((1,), (0,)), ((), ()))
NT = (((1,), (1,)), ((), ()))
TN = (((0,), (0,)), ((), ()))


def dot(a, b, dims=NN, precision=None):
    return lax.dot_general(a, b, dims, precision=precision, preferred_element_type=F32)


class Copies:
    def __init__(self, send, recv):
        self.send, self.recv, self.count, self.sent = send, recv, 0, []

    def post(self, src, dst, to):
        slot = self.count
        self.count += 1
        copy = pltpu.make_async_remote_copy(
            src_ref=src,
            dst_ref=dst,
            send_sem=self.send.at[slot],
            recv_sem=self.recv.at[slot],
            device_id=to,
            device_id_type=pl.DeviceIdType.MESH,
        )
        copy.start()
        self.sent.append(copy)
        return slot

    def same(self, ref, to):
        return self.post(ref, ref, to)

    def arrived(self, slot, ref):
        pltpu.make_async_copy(ref, ref, self.recv.at[slot]).wait()

    def drain(self):
        for copy in self.sent:
            copy.wait_send()
        self.sent = []


class Scatter:
    a0, a1, b0, b1 = slice(0, 32), slice(32, 64), slice(64, 96), slice(96, 128)
    top, low = slice(0, 64), slice(64, 128)

    def __init__(self, net, refs, place, steps, peers):
        self.net = net
        self.parts, self.half_a, self.full_a, self.sum_a, self.half_b, self.full_b, self.sum_b = refs[:7]
        self.half2_a, self.full2_a, self.half2_b, self.full2_b = refs[7:]
        self.x, self.y = place
        self.nx, self.ny = steps
        self.xp, self.xd, self.yp, self.yd = peers

    def multiply(self, rows, weights, two_hops):
        for dy in range(4):
            for dx in range(4):
                if (dx == 2 or dy == 2) == two_hops:
                    yy, xx = self.ny(dy), self.nx(dx)
                    self.parts[yy, xx] = dot(rows, weights[yy * 4 + xx]).astype(BF16)

    def add(self, dst, src):
        dst[...] = (dst[...].astype(F32) + src[...].astype(F32)).astype(BF16)

    def first(self):
        p, nx, ny, post = self.parts, self.nx, self.ny, self.net.post
        self.h = (
            post(p.at[:, nx(2), self.a0], self.half_a.at[0], self.xp),
            post(p.at[:, nx(2), self.a1], self.half_a.at[1], self.xd),
            post(p.at[ny(2), :, self.b0], self.half_b.at[0], self.yp),
            post(p.at[ny(2), :, self.b1], self.half_b.at[1], self.yd),
        )

    def second(self):
        p, nx, ny, post, arrived = self.parts, self.nx, self.ny, self.net.post, self.net.arrived
        arrived(self.h[0], self.half_a.at[0])
        self.add(p.at[:, nx(1), self.a0], self.half_a.at[0])
        f0 = post(p.at[:, nx(1), self.top], self.full_a.at[0], self.xp)
        arrived(self.h[1], self.half_a.at[1])
        self.add(p.at[:, nx(-1), self.a1], self.half_a.at[1])
        f1 = post(p.at[:, nx(-1), self.top], self.full_a.at[1], self.xd)
        arrived(self.h[2], self.half_b.at[0])
        self.add(p.at[ny(1), :, self.b0], self.half_b.at[0])
        f2 = post(p.at[ny(1), :, self.low], self.full_b.at[0], self.yp)
        arrived(self.h[3], self.half_b.at[1])
        self.add(p.at[ny(-1), :, self.b1], self.half_b.at[1])
        f3 = post(p.at[ny(-1), :, self.low], self.full_b.at[1], self.yd)
        self.f = (f0, f1, f2, f3)

    def third(self):
        nx, ny, post, arrived = self.nx, self.ny, self.net.post, self.net.arrived
        arrived(self.f[0], self.full_a.at[0])
        arrived(self.f[1], self.full_a.at[1])
        own = self.parts[:, self.x, self.top].astype(F32)
        self.sum_a[...] = (own + self.full_a[0].astype(F32) + self.full_a[1].astype(F32)).astype(BF16)
        h0 = post(self.sum_a.at[ny(2), self.a0], self.half2_a.at[0], self.yp)
        h1 = post(self.sum_a.at[ny(2), self.a1], self.half2_a.at[1], self.yd)
        arrived(self.f[2], self.full_b.at[0])
        arrived(self.f[3], self.full_b.at[1])
        own = self.parts[self.y, :, self.low].astype(F32)
        self.sum_b[...] = (own + self.full_b[0].astype(F32) + self.full_b[1].astype(F32)).astype(BF16)
        h2 = post(self.sum_b.at[nx(2), self.a0], self.half2_b.at[0], self.xp)
        h3 = post(self.sum_b.at[nx(2), self.a1], self.half2_b.at[1], self.xd)
        self.h = (h0, h1, h2, h3)

    def fourth(self):
        nx, ny, post, arrived = self.nx, self.ny, self.net.post, self.net.arrived
        arrived(self.h[0], self.half2_a.at[0])
        self.add(self.sum_a.at[ny(1), self.a0], self.half2_a.at[0])
        f0 = post(self.sum_a.at[ny(1)], self.full2_a.at[0], self.yp)
        arrived(self.h[1], self.half2_a.at[1])
        self.add(self.sum_a.at[ny(-1), self.a1], self.half2_a.at[1])
        f1 = post(self.sum_a.at[ny(-1)], self.full2_a.at[1], self.yd)
        arrived(self.h[2], self.half2_b.at[0])
        self.add(self.sum_b.at[nx(1), self.a0], self.half2_b.at[0])
        f2 = post(self.sum_b.at[nx(1)], self.full2_b.at[0], self.xp)
        arrived(self.h[3], self.half2_b.at[1])
        self.add(self.sum_b.at[nx(-1), self.a1], self.half2_b.at[1])
        f3 = post(self.sum_b.at[nx(-1)], self.full2_b.at[1], self.xd)
        self.f = (f0, f1, f2, f3)

    def last(self, residual, out, start):
        arrived = self.net.arrived
        for i, (slots, own, full) in enumerate((
            (self.f[:2], self.sum_a.at[self.y], self.full2_a),
            (self.f[2:], self.sum_b.at[self.x], self.full2_b),
        )):
            arrived(slots[0], full.at[0])
            arrived(slots[1], full.at[1])
            mixed = own[...].astype(F32) + full[0].astype(F32) + full[1].astype(F32)
            rows = slice(start + i * 64, start + i * 64 + 64)
            out[rows] = (residual[rows].astype(F32) + mixed).astype(BF16)


def split(v):
    high = v.astype(BF16)
    return high, (v - high.astype(F32)).astype(BF16)


def kernel(*refs):
    dma = pltpu.SemaphoreType.DMA
    pl.run_scoped(functools.partial(layer, *refs), dma((8,)), dma((COPIES,)), dma((COPIES,)))


def layer(
    x_in, wq_in, wk_in, wv_in, wb_in, wo_in, pos_in, mem_in,
    out_ref, memory_ref,
    xg, xn, xm, gv, gq, gk, go, wb_v, pos_v, state, out_v,
    acc_q, acc_k, acc_v, logits, *rest,
):
    sums, (local, send, recv) = rest[:-3], rest[-3:]
    y, x, z, c = (lax.axis_index(n) for n in ("y", "x", "z", "c"))
    ny = lambda d: lax.rem(y + (d % 4), 4)
    nx = lambda d: lax.rem(x + (d % 4), 4)
    nz = lambda d: lax.rem(z + (d % 8), 8)
    up, down = {"z": nz(1)}, {"z": nz(-1)}
    xp, xd = {"x": nx(1)}, {"x": nx(-1)}
    yp, yd = {"y": ny(1)}, {"y": ny(-1)}
    partner = {"c": 1 - c}
    mine = z * 2 + c

    barrier = pltpu.get_barrier_semaphore()
    for peer in (up, down, xp, xd, yp, yd, partner):
        pl.semaphore_signal(barrier, inc=1, device_id=peer, device_id_type=pl.DeviceIdType.MESH)

    loads = [
        (x_in.at[0], xg.at[y, x]),
        (wq_in, gq.at[mine]),
        (wo_in, go.at[mine]),
        (wb_in, wb_v),
        (wv_in, gv.at[mine]),
        (wk_in, gk.at[mine, 0:256]),
        (pos_in.at[0], pos_v),
        (mem_in.at[0], state),
    ]
    fetched = []
    for i, (src, dst) in enumerate(loads):
        copy = pltpu.make_async_copy(src, dst, local.at[i])
        copy.start()
        fetched.append(copy)
    fetched[0].wait()
    with jax.named_scope("enter"):
        pl.semaphore_wait(barrier, 7)
    net = Copies(send, recv)
    same, arrived = net.same, net.arrived

    a0, a1, b0, b1 = slice(0, 64), slice(64, 128), slice(128, 192), slice(192, 256)
    top, low = slice(0, 128), slice(128, 256)
    own_a, own_b = xg.at[y, x, top], xg.at[y, x, low]
    s = [same(own_a, xp), same(own_a, xd), same(own_b, yp), same(own_b, yd)]

    from_down, from_up, from_partner = {}, {}, {}
    Q, O, V, K = range(4)
    bufs = (gq, go, gv, gk)

    def block(d):
        return nz(d) * 2 + c

    def give(m, *distances):
        for d in distances:
            from_partner[m, d] = same(bufs[m].at[block(d)], partner)

    def send_own(m):
        from_down[m] = same(bufs[m].at[block(0)], up)
        from_up[m] = same(bufs[m].at[block(0)], down)

    def relay(m, d):
        arrived(from_down[m], bufs[m].at[block(-d)])
        from_down[m] = same(bufs[m].at[block(-d)], up)
        arrived(from_up[m], bufs[m].at[block(d)])
        from_up[m] = same(bufs[m].at[block(d)], down)

    def relay_half(m):
        rest = slice(128, bufs[m].shape[1])
        arrived(from_down[m], bufs[m].at[block(-3)])
        from_down[m] = same(bufs[m].at[block(-3), top], up)
        arrived(from_up[m], bufs[m].at[block(3)])
        from_up[m] = same(bufs[m].at[block(3), rest], down)

    def far(m):
        rest = slice(128, bufs[m].shape[1])
        arrived(from_down[m], bufs[m].at[block(4), top])
        arrived(from_up[m], bufs[m].at[block(4), rest])
        give(m, 4)

    def take(m, *distances):
        for d in distances:
            arrived(from_partner[m, d], bufs[m].at[nz(d) * 2 + (1 - c)])

    fetched[1].wait()
    send_own(Q)
    fetched[2].wait()
    send_own(O)
    give(Q, 0)
    give(O, 0)
    for copy in fetched[3:]:
        copy.wait()
    rows = jnp.concatenate([wb_v[...].astype(F32), jnp.zeros((14, 256), F32)], axis=0)
    gk[mine, 256:272, :] = rows.astype(BF16)
    acc_q[...] = jnp.zeros_like(acc_q)
    acc_k[...] = jnp.zeros_like(acc_k)
    acc_v[...] = jnp.zeros_like(acc_v)
    logits[...] = jnp.zeros_like(logits)
    row = lax.broadcasted_iota(jnp.int32, (256, 128), 0)
    where = jnp.concatenate([pos_v[0:1, :], pos_v[1:2, :] + 128], axis=1)
    chosen = jnp.where(row == where, 1.0, 0.0).T.astype(BF16)

    arrived(s[0], xg.at[y, nx(-1), top])
    f0 = same(xg.at[y, nx(-1), a0], xp)
    arrived(s[1], xg.at[y, nx(1), top])
    f1 = same(xg.at[y, nx(1), a1], xd)
    arrived(s[2], xg.at[ny(-1), x, low])
    f2 = same(xg.at[ny(-1), x, b0], yp)
    arrived(s[3], xg.at[ny(1), x, low])
    f3 = same(xg.at[ny(1), x, b1], yd)
    relay(Q, 1)
    arrived(f0, xg.at[y, nx(2), a0])
    arrived(f1, xg.at[y, nx(2), a1])
    rows_a = lambda yy, r: xg.at[yy, :, r]
    s0 = same(rows_a(y, top), yp)
    s1 = same(rows_a(y, top), yd)
    arrived(f2, xg.at[ny(2), x, b0])
    arrived(f3, xg.at[ny(2), x, b1])
    rows_b = lambda xx, r: xg.at[:, xx, r]
    s2 = same(rows_b(x, low), xp)
    s3 = same(rows_b(x, low), xd)
    give(Q, -1, 1)
    relay(O, 1)
    give(O, -1, 1)
    relay(Q, 2)
    give(Q, -2, 2)

    arrived(s0, rows_a(ny(-1), top))
    f0 = same(rows_a(ny(-1), a0), yp)
    arrived(s1, rows_a(ny(1), top))
    f1 = same(rows_a(ny(1), a1), yd)
    arrived(s2, rows_b(nx(-1), low))
    f2 = same(rows_b(nx(-1), b0), xp)
    arrived(s3, rows_b(nx(1), low))
    f3 = same(rows_b(nx(1), b1), xd)
    relay(O, 2)
    send_own(V)
    send_own(K)
    give(O, -2, 2)
    give(V, 0)
    give(K, 0)
    relay_half(Q)
    give(Q, -3, 3)
    arrived(f0, rows_a(ny(2), a0))
    arrived(f1, rows_a(ny(2), a1))
    arrived(f2, rows_b(nx(2), b0))
    arrived(f3, rows_b(nx(2), b1))

    def squares(i, total):
        v = xg[i // 4, lax.rem(i, 4)].astype(F32)
        v = v * v
        return total + (v[:, 0:128] + v[:, 128:256])

    with jax.named_scope("squares"):
        total = lax.fori_loop(0, 16, squares, jnp.zeros((256, 128), F32))
        scale = lax.rsqrt(jnp.sum(total, axis=1, keepdims=True) * (1.0 / 4096) + EPS)
    relay_half(O)
    give(O, -3, 3)

    def normalise(i, carry):
        v = xg[i // 4, lax.rem(i, 4)].astype(F32)
        n = (v * scale).astype(BF16)
        xn[i] = n
        xm[i] = dot(chosen, n).astype(BF16)
        return carry

    with jax.named_scope("normalise"):
        lax.fori_loop(0, 16, normalise, 0)

    def project(m, *distances):
        take(m, *distances)
        acc = {Q: acc_q, V: acc_v, K: acc_k}[m]
        left = xn if m == Q else xm
        for d in distances:
            i = nz(d) * 2
            acc[...] += dot(left[i], bufs[m][i, 0:256]) + dot(left[i + 1], bufs[m][i + 1, 0:256])
            if m == K:
                extra = slice(256, 272)
                logits[...] += dot(left[i], gk[i, extra], NT) + dot(left[i + 1], gk[i + 1, extra], NT)

    relay(V, 1)
    give(V, -1, 1)
    with jax.named_scope("project_q"):
        project(Q, 0, -1, 1, -2, 2, -3, 3)
    relay(K, 1)
    give(K, -1, 1)
    far(Q)
    far(O)
    project(Q, 4)

    def wide_state(h):
        high, lo = split(state[h])
        return jnp.concatenate([high, lo, high], axis=1)

    def through(rows, wide):
        high, lo = split(rows)
        return dot(jnp.concatenate([high, high, lo], axis=1), wide, NT)

    cols = (slice(0, 128), slice(128, 256))
    seg_rows = (slice(0, 128), slice(128, 256))
    seg_mem = (slice(0, 64), slice(64, 128))

    def queries(seg, h):
        return acc_q[seg_rows[seg], cols[h]] * (128.0 ** -0.5)

    wides = [wide_state(h) for h in range(2)]
    readout = jnp.concatenate([through(queries(0, h), wides[h]) for h in range(2)], axis=1).astype(BF16)
    take(O, 0, -1, 1, -2, 2, -3, 3, 4)
    scatter = [
        Scatter(net, [r.at[seg] for r in sums], (x, y), (nx, ny), (xp, xd, yp, yd)) for seg in range(2)
    ]
    with jax.named_scope("multiply0"):
        scatter[0].multiply(readout, go, True)
        scatter[0].first()
        scatter[0].multiply(readout, go, False)
    relay(V, 2)
    give(V, -2, 2)
    project(V, 0, -1, 1)
    scatter[0].second()
    relay(K, 2)
    give(K, -2, 2)
    project(K, 0, -1, 1)
    relay_half(V)
    give(V, -3, 3)
    scatter[0].third()
    relay_half(K)
    give(K, -3, 3)
    project(V, -2, 2)
    project(K, -2, 2)
    far(V)
    scatter[0].fourth()
    project(V, -3, 3)
    far(K)
    project(K, -3, 3)
    project(V, 4)
    project(K, 4)

    keys, values, betas = [], [], []
    for h in range(2):
        k = acc_k[:, cols[h]]
        keys.append(k * lax.rsqrt(jnp.sum(k * k, axis=1, keepdims=True) + 1e-06))
        values.append(acc_v[:, cols[h]])
        betas.append(jax.nn.sigmoid(logits[:, h:h + 1]))

    def update(seg, h, recalled):
        m = seg_mem[seg]
        ch, cl = split(betas[h][m] * (values[h][m] - recalled))
        kh, kl = split(keys[h][m])
        state[h] += dot(jnp.concatenate([ch, ch, cl], axis=0), jnp.concatenate([kh, kl, kh], axis=0), TN)

    with jax.named_scope("recur"):
        for h in range(2):
            update(0, h, through(keys[h][seg_mem[0]], wide_state(h)))
        got = []
        for h in range(2):
            got.append(through(jnp.concatenate([queries(1, h), keys[h][seg_mem[1]]], axis=0), wide_state(h)))
        readout = jnp.concatenate([g[0:128] for g in got], axis=1).astype(BF16)
    with jax.named_scope("multiply1"):
        scatter[1].multiply(readout, go, True)
        scatter[1].first()
        scatter[1].multiply(readout, go, False)

    for h in range(2):
        update(1, h, got[h][128:192])
    stored = []
    for h in range(2):
        copy = pltpu.make_async_copy(state.at[h], memory_ref.at[0, h], local.at[h])
        copy.start()
        stored.append(copy)

    def put_out(seg):
        scatter[seg].last(xg.at[y, x], out_v, seg * 128)
        part = seg_rows[seg]
        copy = pltpu.make_async_copy(out_v.at[part], out_ref.at[0, part], local.at[2 + seg])
        copy.start()
        stored.append(copy)

    put_out(0)
    scatter[1].second()
    scatter[1].third()
    scatter[1].fourth()
    put_out(1)
    with jax.named_scope("drain"):
        net.drain()
    with jax.named_scope("stored"):
        for copy in stored:
            copy.wait()


COPIES = 112


def body(hidden_in, w_query, w_key, w_value, w_beta, w_out, mem_pos, memory_in):
    vmem = pltpu.VMEM
    scratch = [
        vmem((4, 4, 256, 256), BF16),
        vmem((16, 256, 256), BF16),
        vmem((16, 128, 256), BF16),
        vmem((16, 256, 256), BF16),
        vmem((16, 256, 256), BF16),
        vmem((16, 272, 256), BF16),
        vmem((16, 256, 256), BF16),
        vmem((2, 256), BF16),
        vmem((2, 64), jnp.int32),
        vmem((2, 128, 128), F32),
        vmem((256, 256), BF16),
        vmem((256, 256), F32),
        vmem((128, 256), F32),
        vmem((128, 256), F32),
        vmem((128, 16), F32),
        vmem((2, 4, 4, 128, 256), BF16),
        vmem((2, 2, 4, 32, 256), BF16),
        vmem((2, 2, 4, 64, 256), BF16),
        vmem((2, 4, 64, 256), BF16),
        vmem((2, 2, 4, 32, 256), BF16),
        vmem((2, 2, 4, 64, 256), BF16),
        vmem((2, 4, 64, 256), BF16),
        vmem((2, 2, 32, 256), BF16),
        vmem((2, 2, 64, 256), BF16),
        vmem((2, 2, 32, 256), BF16),
        vmem((2, 2, 64, 256), BF16),
    ]
    return pl.pallas_call(
        kernel,
        out_shape=(
            jax.ShapeDtypeStruct(hidden_in.shape, BF16),
            jax.ShapeDtypeStruct(memory_in.shape, F32),
        ),
        in_specs=[pl.BlockSpec(memory_space=pltpu.HBM)] * 8,
        out_specs=[pl.BlockSpec(memory_space=pltpu.HBM)] * 2,
        scratch_shapes=scratch,
        compiler_params=pltpu.CompilerParams(
            collective_id=0, has_side_effects=True
        ),
    )(hidden_in, w_query, w_key, w_value, w_beta.T, w_out, mem_pos, memory_in)


def solution(mesh):
    split = Mesh(mesh.devices.reshape(4, 4, 8, 2), ("y", "x", "z", "c"))
    return jax.shard_map(
        body,
        mesh=split,
        in_specs=(
            P(BATCH, None, HEAD),
            P(BATCH, HEAD),
            P(BATCH, HEAD),
            P(BATCH, HEAD),
            P(BATCH, HEAD),
            P(HEAD, BATCH),
            P(BATCH, None, None),
            P(BATCH, HEAD, None, None),
        ),
        out_specs=(P(BATCH, None, HEAD), P(BATCH, HEAD, None, None)),
        check_vma=False,
    )
```

time: 89 us -> 73.7 us (0.83)
  Pallas kernels: 85.9 us -> 70 us
    pallas_call x1, Pallas kernels: 85.9 us -> 70 us  [body(): pl.pallas_call(kernel, out_shape=(jax.ShapeDtypeStruct(hidden_in.shape, B...]
where the time goes in v2:
time: 73.7 us; the launch traced here: 72.9 us
  Pallas kernels  70 us (95%)
  local copies, waits for them, and re-layouts  2.26 us (3%)
    pallas_call x1, Pallas kernels, body(): pl.pallas_call(kernel, out_shape=(jax.ShapeDtypeStruct(hidden_in.shape, B...  70 us
    unnamed x4, local copies, waits for them, and re-layouts  2.26 us

profile of v2, /device:TPU:1, one launch (start us, length us, event | category | flops | bytes accessed | tf_op | source)
XLA Modules:
  0.0 72.9 jit_solution(9409636506422014349)
XLA Ops:
  0.6 70.0 %shard_map.95 = (bf16[1,256,256]{2,1,0:T(8,128)(2,1)}, f32[1,2,128,128]{3,2,1,0:T(8,128)}) custom-call(bf16[1,256,256]{2,1,0:T(8,128)(2,1)} %refs_0_.1, bf16[256,256]{1,0:T(8,128)(2,1)} %refs_1_.1, bf16[256,256]{1,0:T(8,128)(2,1)} %refs_2_.1, bf16[256,256]{1,0:T(8,128)(2,1)} %refs_3_.1, bf16[2,256]{1,0:T(2,128)(2,1)} %bitcast.1, bf16[256,256]{1,0:T(8,128)(2,1)} %refs_5_.1, ...), custom_call_target="tpu_custom_call" | custom-call | tf_op jit(solution)/shard_map/pallas_call | solution.py:482
  70.6 0.0 copy-start
  70.6 1.6 %copy.12 = bf16[1,256,256]{2,1,0:T(8,128)(2,1)} copy(bf16[1,256,256]{2,1,0:T(8,128)(2,1)} %get-tuple-element.4) | data formatting | bytes 262144
  72.2 0.0 copy-done
  72.2 0.7 copy.13
Async XLA Ops:
  70.6 1.6 %copy-start = (f32[1,2,128,128]{3,2,1,0:T(8,128)S(1)}, f32[1,2,128,128]{3,2,1,0:T(8,128)}, u32[]{:S(2)}) copy-start(f32[1,2,128,128]{3,2,1,0:T(8,128)} %get-tuple-element.5) | copy-start | bytes 393220

commit v3 on v2

--- a/solution.py
+++ b/solution.py
@@ -60,89 +60,77 @@
 
     def __init__(self, net, refs, place, steps, peers):
         self.net = net
-        self.parts, self.half_a, self.full_a, self.sum_a, self.half_b, self.full_b, self.sum_b = refs[:7]
-        self.half2_a, self.full2_a, self.half2_b, self.full2_b = refs[7:]
+        self.parts, self.half_a, self.far_a, self.full_a, self.sum_a, self.end_a = refs[:6]
+        self.half_b, self.far_b, self.full_b, self.sum_b, self.end_b = refs[6:]
         self.x, self.y = place
         self.nx, self.ny = steps
-        self.xp, self.xd, self.yp, self.yd = peers
-
-    def multiply(self, rows, weights, two_hops):
+        self.xp, self.xd, self.yp, self.yd, self.x2, self.y2 = peers
+
+    def multiply(self, rows, weights, hops):
         for dy in range(4):
             for dx in range(4):
-                if (dx == 2 or dy == 2) == two_hops:
+                if max((0, 1, 2, 1)[dx], (0, 1, 2, 1)[dy]) == hops:
                     yy, xx = self.ny(dy), self.nx(dx)
                     self.parts[yy, xx] = dot(rows, weights[yy * 4 + xx]).astype(BF16)
 
-    def add(self, dst, src):
-        dst[...] = (dst[...].astype(F32) + src[...].astype(F32)).astype(BF16)
-
-    def first(self):
+    def start(self, rows, weights):
         p, nx, ny, post = self.parts, self.nx, self.ny, self.net.post
+        self.multiply(rows, weights, 2)
         self.h = (
             post(p.at[:, nx(2), self.a0], self.half_a.at[0], self.xp),
             post(p.at[:, nx(2), self.a1], self.half_a.at[1], self.xd),
             post(p.at[ny(2), :, self.b0], self.half_b.at[0], self.yp),
             post(p.at[ny(2), :, self.b1], self.half_b.at[1], self.yd),
         )
-
-    def second(self):
-        p, nx, ny, post, arrived = self.parts, self.nx, self.ny, self.net.post, self.net.arrived
-        arrived(self.h[0], self.half_a.at[0])
-        self.add(p.at[:, nx(1), self.a0], self.half_a.at[0])
-        f0 = post(p.at[:, nx(1), self.top], self.full_a.at[0], self.xp)
-        arrived(self.h[1], self.half_a.at[1])
-        self.add(p.at[:, nx(-1), self.a1], self.half_a.at[1])
-        f1 = post(p.at[:, nx(-1), self.top], self.full_a.at[1], self.xd)
-        arrived(self.h[2], self.half_b.at[0])
-        self.add(p.at[ny(1), :, self.b0], self.half_b.at[0])
-        f2 = post(p.at[ny(1), :, self.low], self.full_b.at[0], self.yp)
-        arrived(self.h[3], self.half_b.at[1])
-        self.add(p.at[ny(-1), :, self.b1], self.half_b.at[1])
-        f3 = post(p.at[ny(-1), :, self.low], self.full_b.at[1], self.yd)
-        self.f = (f0, f1, f2, f3)
-
-    def third(self):
-        nx, ny, post, arrived = self.nx, self.ny, self.net.post, self.net.arrived
-        arrived(self.f[0], self.full_a.at[0])
-        arrived(self.f[1], self.full_a.at[1])
-        own = self.parts[:, self.x, self.top].astype(F32)
-        self.sum_a[...] = (own + self.full_a[0].astype(F32) + self.full_a[1].astype(F32)).astype(BF16)
-        h0 = post(self.sum_a.at[ny(2), self.a0], self.half2_a.at[0], self.yp)
-        h1 = post(self.sum_a.at[ny(2), self.a1], self.half2_a.at[1], self.yd)
-        arrived(self.f[2], self.full_b.at[0])
-        arrived(self.f[3], self.full_b.at[1])
-        own = self.parts[self.y, :, self.low].astype(F32)
-        self.sum_b[...] = (own + self.full_b[0].astype(F32) + self.full_b[1].astype(F32)).astype(BF16)
-        h2 = post(self.sum_b.at[nx(2), self.a0], self.half2_b.at[0], self.xp)
-        h3 = post(self.sum_b.at[nx(2), self.a1], self.half2_b.at[1], self.xd)
-        self.h = (h0, h1, h2, h3)
-
-    def fourth(self):
-        nx, ny, post, arrived = self.nx, self.ny, self.net.post, self.net.arrived
-        arrived(self.h[0], self.half2_a.at[0])
-        self.add(self.sum_a.at[ny(1), self.a0], self.half2_a.at[0])
-        f0 = post(self.sum_a.at[ny(1)], self.full2_a.at[0], self.yp)
-        arrived(self.h[1], self.half2_a.at[1])
-        self.add(self.sum_a.at[ny(-1), self.a1], self.half2_a.at[1])
-        f1 = post(self.sum_a.at[ny(-1)], self.full2_a.at[1], self.yd)
-        arrived(self.h[2], self.half2_b.at[0])
-        self.add(self.sum_b.at[nx(1), self.a0], self.half2_b.at[0])
-        f2 = post(self.sum_b.at[nx(1)], self.full2_b.at[0], self.xp)
-        arrived(self.h[3], self.half2_b.at[1])
-        self.add(self.sum_b.at[nx(-1), self.a1], self.half2_b.at[1])
-        f3 = post(self.sum_b.at[nx(-1)], self.full2_b.at[1], self.xd)
-        self.f = (f0, f1, f2, f3)
+        self.multiply(rows, weights, 1)
+        self.f = (
+            post(p.at[:, nx(1), self.top], self.full_a.at[0], self.xp),
+            post(p.at[:, nx(-1), self.top], self.full_a.at[1], self.xd),
+            post(p.at[ny(1), :, self.low], self.full_b.at[0], self.yp),
+            post(p.at[ny(-1), :, self.low], self.full_b.at[1], self.yd),
+        )
+        self.multiply(rows, weights, 0)
+
+    def hand_on(self):
+        passed = []
+        for slot, (half, far, i, to) in zip(self.h, (
+            (self.half_a, self.far_a, 0, self.xp),
+            (self.half_a, self.far_a, 1, self.xd),
+            (self.half_b, self.far_b, 0, self.yp),
+            (self.half_b, self.far_b, 1, self.yd),
+        )):
+            self.net.arrived(slot, half.at[i])
+            passed.append(self.net.post(half.at[i], far.at[i], to))
+        self.h = passed
+
+    def turn(self):
+        arrived, post = self.net.arrived, self.net.post
+        self.e = []
+        for j, (own, full, far, total, end, step, peers) in enumerate((
+            (self.parts.at[:, self.x, self.top], self.full_a, self.far_a, self.sum_a, self.end_a, self.ny,
+             (self.yp, self.yd, self.y2)),
+            (self.parts.at[self.y, :, self.low], self.full_b, self.far_b, self.sum_b, self.end_b, self.nx,
+             (self.xp, self.xd, self.x2)),
+        )):
+            for i in range(2):
+                arrived(self.f[2 * j + i], full.at[i])
+            near = own[...].astype(F32) + full[0].astype(F32) + full[1].astype(F32)
+            for i in range(2):
+                arrived(self.h[2 * j + i], far.at[i])
+            total[:, 0:32] = (near[:, 0:32] + far[0].astype(F32)).astype(BF16)
+            total[:, 32:64] = (near[:, 32:64] + far[1].astype(F32)).astype(BF16)
+            self.e.append([
+                post(total.at[step(d)], end.at[i], to)
+                for i, (d, to) in reversed(tuple(enumerate(zip((1, -1, 2), peers))))
+            ][::-1])
 
     def last(self, residual, out, start):
-        arrived = self.net.arrived
-        for i, (slots, own, full) in enumerate((
-            (self.f[:2], self.sum_a.at[self.y], self.full2_a),
-            (self.f[2:], self.sum_b.at[self.x], self.full2_b),
-        )):
-            arrived(slots[0], full.at[0])
-            arrived(slots[1], full.at[1])
-            mixed = own[...].astype(F32) + full[0].astype(F32) + full[1].astype(F32)
-            rows = slice(start + i * 64, start + i * 64 + 64)
+        for j, (own, end) in enumerate(((self.sum_a.at[self.y], self.end_a), (self.sum_b.at[self.x], self.end_b))):
+            mixed = own[...].astype(F32)
+            for i in range(3):
+                self.net.arrived(self.e[j][i], end.at[i])
+                mixed += end[i].astype(F32)
+            rows = slice(start + j * 64, start + j * 64 + 64)
             out[rows] = (residual[rows].astype(F32) + mixed).astype(BF16)
 
 
@@ -174,7 +162,8 @@
     mine = z * 2 + c
 
     barrier = pltpu.get_barrier_semaphore()
-    for peer in (up, down, xp, xd, yp, yd, partner):
+    x2, y2 = {"x": nx(2)}, {"y": ny(2)}
+    for peer in (up, down, xp, xd, yp, yd, x2, y2, partner):
         pl.semaphore_signal(barrier, inc=1, device_id=peer, device_id_type=pl.DeviceIdType.MESH)
 
     loads = [
@@ -194,7 +183,7 @@
         fetched.append(copy)
     fetched[0].wait()
     with jax.named_scope("enter"):
-        pl.semaphore_wait(barrier, 7)
+        pl.semaphore_wait(barrier, 9)
     net = Copies(send, recv)
     same, arrived = net.same, net.arrived
 
@@ -366,28 +355,25 @@
     readout = jnp.concatenate([through(queries(0, h), wides[h]) for h in range(2)], axis=1).astype(BF16)
     take(O, 0, -1, 1, -2, 2, -3, 3, 4)
     scatter = [
-        Scatter(net, [r.at[seg] for r in sums], (x, y), (nx, ny), (xp, xd, yp, yd)) for seg in range(2)
+        Scatter(net, [r.at[seg] for r in sums], (x, y), (nx, ny), (xp, xd, yp, yd, x2, y2)) for seg in range(2)
     ]
     with jax.named_scope("multiply0"):
-        scatter[0].multiply(readout, go, True)
-        scatter[0].first()
-        scatter[0].multiply(readout, go, False)
+        scatter[0].start(readout, go)
     relay(V, 2)
     give(V, -2, 2)
     project(V, 0, -1, 1)
-    scatter[0].second()
+    scatter[0].hand_on()
     relay(K, 2)
     give(K, -2, 2)
     project(K, 0, -1, 1)
     relay_half(V)
     give(V, -3, 3)
-    scatter[0].third()
+    scatter[0].turn()
     relay_half(K)
     give(K, -3, 3)
     project(V, -2, 2)
     project(K, -2, 2)
     far(V)
-    scatter[0].fourth()
     project(V, -3, 3)
     far(K)
     project(K, -3, 3)
@@ -415,9 +401,7 @@
             got.append(through(jnp.concatenate([queries(1, h), keys[h][seg_mem[1]]], axis=0), wide_state(h)))
         readout = jnp.concatenate([g[0:128] for g in got], axis=1).astype(BF16)
     with jax.named_scope("multiply1"):
-        scatter[1].multiply(readout, go, True)
-        scatter[1].first()
-        scatter[1].multiply(readout, go, False)
+        scatter[1].start(readout, go)
 
     for h in range(2):
         update(1, h, got[h][128:192])
@@ -434,10 +418,9 @@
         copy.start()
         stored.append(copy)
 
+    scatter[1].hand_on()
     put_out(0)
-    scatter[1].second()
-    scatter[1].third()
-    scatter[1].fourth()
+    scatter[1].turn()
     put_out(1)
     with jax.named_scope("drain"):
         net.drain()
@@ -446,7 +429,7 @@
             copy.wait()
 
 
-COPIES = 112
+COPIES = 116
 
 
 def body(hidden_in, w_query, w_key, w_value, w_beta, w_out, mem_pos, memory_in):
@@ -469,15 +452,15 @@
         vmem((128, 16), F32),
         vmem((2, 4, 4, 128, 256), BF16),
         vmem((2, 2, 4, 32, 256), BF16),
-        vmem((2, 2, 4, 64, 256), BF16),
-        vmem((2, 4, 64, 256), BF16),
         vmem((2, 2, 4, 32, 256), BF16),
         vmem((2, 2, 4, 64, 256), BF16),
         vmem((2, 4, 64, 256), BF16),
-        vmem((2, 2, 32, 256), BF16),
-        vmem((2, 2, 64, 256), BF16),
-        vmem((2, 2, 32, 256), BF16),
-        vmem((2, 2, 64, 256), BF16),
+        vmem((2, 3, 64, 256), BF16),
+        vmem((2, 2, 4, 32, 256), BF16),
+        vmem((2, 2, 4, 32, 256), BF16),
+        vmem((2, 2, 4, 64, 256), BF16),
+        vmem((2, 4, 64, 256), BF16),
+        vmem((2, 3, 64, 256), BF16),
     ]
     return pl.pallas_call(
         kernel,

time: 73.7 us -> 71.3 us (0.967)
  Pallas kernels: 70 us -> 68.3 us
    pallas_call x1, Pallas kernels: 70 us -> 68.3 us  [body(): pl.pallas_call(kernel, out_shape=(jax.ShapeDtypeStruct(hidden_in.shape, B...]
where the time goes in v3:
time: 71.3 us; the launch traced here: 71.2 us
  Pallas kernels  68.3 us (96%)
  local copies, waits for them, and re-layouts  2.26 us (3%)
    pallas_call x1, Pallas kernels, body(): pl.pallas_call(kernel, out_shape=(jax.ShapeDtypeStruct(hidden_in.shape, B...  68.3 us
    unnamed x4, local copies, waits for them, and re-layouts  2.26 us

profile of v3, /device:TPU:1, one launch (start us, length us, event | category | flops | bytes accessed | tf_op | source)
XLA Modules:
  0.0 71.2 jit_solution(18325384612499261925)
XLA Ops:
  0.6 68.3 %shard_map.95 = (bf16[1,256,256]{2,1,0:T(8,128)(2,1)}, f32[1,2,128,128]{3,2,1,0:T(8,128)}) custom-call(bf16[1,256,256]{2,1,0:T(8,128)(2,1)} %refs_0_.1, bf16[256,256]{1,0:T(8,128)(2,1)} %refs_1_.1, bf16[256,256]{1,0:T(8,128)(2,1)} %refs_2_.1, bf16[256,256]{1,0:T(8,128)(2,1)} %refs_3_.1, bf16[2,256]{1,0:T(2,128)(2,1)} %bitcast.1, bf16[256,256]{1,0:T(8,128)(2,1)} %refs_5_.1, ...), custom_call_target="tpu_custom_call" | custom-call | tf_op jit(solution)/shard_map/pallas_call | solution.py:465
  68.9 0.0 copy-start
  68.9 1.6 %copy.12 = bf16[1,256,256]{2,1,0:T(8,128)(2,1)} copy(bf16[1,256,256]{2,1,0:T(8,128)(2,1)} %get-tuple-element.4) | data formatting | bytes 262144
  70.5 0.0 copy-done
  70.5 0.7 copy.13
Async XLA Ops:
  68.9 1.6 %copy-start = (f32[1,2,128,128]{3,2,1,0:T(8,128)S(1)}, f32[1,2,128,128]{3,2,1,0:T(8,128)}, u32[]{:S(2)}) copy-start(f32[1,2,128,128]{3,2,1,0:T(8,128)} %get-tuple-element.5) | copy-start | bytes 393220

commit v4 on v3

--- a/solution.py
+++ b/solution.py
@@ -25,7 +25,7 @@
 
 class Copies:
     def __init__(self, send, recv):
-        self.send, self.recv, self.count, self.sent = send, recv, 0, []
+        self.send, self.recv, self.count, self.sent = send, recv, 0, {}
 
     def post(self, src, dst, to):
         slot = self.count
@@ -39,7 +39,7 @@
             device_id_type=pl.DeviceIdType.MESH,
         )
         copy.start()
-        self.sent.append(copy)
+        self.sent[slot] = copy
         return slot
 
     def same(self, ref, to):
@@ -48,85 +48,82 @@
     def arrived(self, slot, ref):
         pltpu.make_async_copy(ref, ref, self.recv.at[slot]).wait()
 
+    def gone(self, slot):
+        self.sent.pop(slot).wait_send()
+
     def drain(self):
-        for copy in self.sent:
-            copy.wait_send()
-        self.sent = []
+        for slot in tuple(self.sent):
+            self.gone(slot)
 
 
 class Scatter:
-    a0, a1, b0, b1 = slice(0, 32), slice(32, 64), slice(64, 96), slice(96, 128)
-    top, low = slice(0, 64), slice(64, 128)
-
-    def __init__(self, net, refs, place, steps, peers):
-        self.net = net
-        self.parts, self.half_a, self.far_a, self.full_a, self.sum_a, self.end_a = refs[:6]
-        self.half_b, self.far_b, self.full_b, self.sum_b, self.end_b = refs[6:]
-        self.x, self.y = place
-        self.nx, self.ny = steps
-        self.xp, self.xd, self.yp, self.yd, self.x2, self.y2 = peers
+    HOPS = (2, 1, 3, 0)
+
+    def __init__(self, net, refs, steps, peers):
+        self.net, self.steps = net, steps
+        self.sides = tuple(zip((refs[:7], refs[7:]), (peers[:3], peers[3:]), (peers[3:], peers[:3])))
 
     def multiply(self, rows, weights, hops):
+        (pa, *_), (pb, *_) = (side[0] for side in self.sides)
+        nx, ny = self.steps
         for dy in range(4):
             for dx in range(4):
                 if max((0, 1, 2, 1)[dx], (0, 1, 2, 1)[dy]) == hops:
-                    yy, xx = self.ny(dy), self.nx(dx)
-                    self.parts[yy, xx] = dot(rows, weights[yy * 4 + xx]).astype(BF16)
+                    got = dot(rows, weights[ny(dy) * 4 + nx(dx)]).astype(BF16)
+                    pa[dx, self.HOPS.index(dy)] = got[0:64]
+                    pb[dy, self.HOPS.index(dx)] = got[64:128]
 
     def start(self, rows, weights):
-        p, nx, ny, post = self.parts, self.nx, self.ny, self.net.post
         self.multiply(rows, weights, 2)
-        self.h = (
-            post(p.at[:, nx(2), self.a0], self.half_a.at[0], self.xp),
-            post(p.at[:, nx(2), self.a1], self.half_a.at[1], self.xd),
-            post(p.at[ny(2), :, self.b0], self.half_b.at[0], self.yp),
-            post(p.at[ny(2), :, self.b1], self.half_b.at[1], self.yd),
-        )
+        self.h = []
+        for (p, half, *_), to, _ in self.sides:
+            for i in range(2):
+                self.h.append(self.net.post(p.at[2, :, 32 * i:32 * i + 32], half.at[i], to[i]))
         self.multiply(rows, weights, 1)
-        self.f = (
-            post(p.at[:, nx(1), self.top], self.full_a.at[0], self.xp),
-            post(p.at[:, nx(-1), self.top], self.full_a.at[1], self.xd),
-            post(p.at[ny(1), :, self.low], self.full_b.at[0], self.yp),
-            post(p.at[ny(-1), :, self.low], self.full_b.at[1], self.yd),
-        )
         self.multiply(rows, weights, 0)
 
+    def push(self, wait):
+        if wait:
+            for slot in self.h:
+                self.net.gone(slot)
+        self.f = []
+        for part in (slice(0, 1), slice(1, 4)):
+            for (p, _, _, full, *_), to, _ in self.sides:
+                for i in range(2):
+                    self.f.append(self.net.post(p.at[1 + 2 * i, part], full.at[i, part], to[i]))
+
     def hand_on(self):
-        passed = []
-        for slot, (half, far, i, to) in zip(self.h, (
-            (self.half_a, self.far_a, 0, self.xp),
-            (self.half_a, self.far_a, 1, self.xd),
-            (self.half_b, self.far_b, 0, self.yp),
-            (self.half_b, self.far_b, 1, self.yd),
-        )):
-            self.net.arrived(slot, half.at[i])
-            passed.append(self.net.post(half.at[i], far.at[i], to))
-        self.h = passed
+        early, late = [], []
+        for j, ((_, half, far, *_), to, _) in enumerate(self.sides):
+            for i in range(2):
+                self.net.arrived(self.h[2 * j + i], half.at[i])
+                early.append(self.net.post(half.at[i, 0:1], far.at[i, 0:1], to[i]))
+                late.append(self.net.post(half.at[i, 1:4], far.at[i, 1:4], to[i]))
+        self.h = early + late
 
     def turn(self):
-        arrived, post = self.net.arrived, self.net.post
-        self.e = []
-        for j, (own, full, far, total, end, step, peers) in enumerate((
-            (self.parts.at[:, self.x, self.top], self.full_a, self.far_a, self.sum_a, self.end_a, self.ny,
-             (self.yp, self.yd, self.y2)),
-            (self.parts.at[self.y, :, self.low], self.full_b, self.far_b, self.sum_b, self.end_b, self.nx,
-             (self.xp, self.xd, self.x2)),
-        )):
-            for i in range(2):
-                arrived(self.f[2 * j + i], full.at[i])
-            near = own[...].astype(F32) + full[0].astype(F32) + full[1].astype(F32)
-            for i in range(2):
-                arrived(self.h[2 * j + i], far.at[i])
-            total[:, 0:32] = (near[:, 0:32] + far[0].astype(F32)).astype(BF16)
-            total[:, 32:64] = (near[:, 32:64] + far[1].astype(F32)).astype(BF16)
-            self.e.append([
-                post(total.at[step(d)], end.at[i], to)
-                for i, (d, to) in reversed(tuple(enumerate(zip((1, -1, 2), peers))))
-            ][::-1])
+        self.e = [[], []]
+        for late, part in enumerate((slice(0, 1), slice(1, 4))):
+            for j, ((p, _, far, full, total, own, end), _, peers) in enumerate(self.sides):
+                for i in range(2):
+                    self.net.arrived(self.f[4 * late + 2 * j + i], full.at[i, part])
+                near = p[0, part].astype(F32) + full[0, part].astype(F32) + full[1, part].astype(F32)
+                for i in range(2):
+                    self.net.arrived(self.h[4 * late + 2 * j + i], far.at[i, part])
+                passed = jnp.concatenate([far[0, part].astype(F32), far[1, part].astype(F32)], axis=1)
+                near = near + passed
+                if late:
+                    total[1:3] = near[0:2].astype(BF16)
+                    own[...] = near[2]
+                    self.e[j].append(self.net.post(total.at[1], end.at[1], peers[0]))
+                    self.e[j].append(self.net.post(total.at[2], end.at[2], peers[1]))
+                else:
+                    total[0:1] = near.astype(BF16)
+                    self.e[j].append(self.net.post(total.at[0], end.at[0], peers[2]))
 
     def last(self, residual, out, start):
-        for j, (own, end) in enumerate(((self.sum_a.at[self.y], self.end_a), (self.sum_b.at[self.x], self.end_b))):
-            mixed = own[...].astype(F32)
+        for j, ((*_, own, end), _, _) in enumerate(self.sides):
+            mixed = own[...]
             for i in range(3):
                 self.net.arrived(self.e[j][i], end.at[i])
                 mixed += end[i].astype(F32)
@@ -170,8 +167,8 @@
         (x_in.at[0], xg.at[y, x]),
         (wq_in, gq.at[mine]),
         (wo_in, go.at[mine]),
+        (wv_in, gv.at[mine]),
         (wb_in, wb_v),
-        (wv_in, gv.at[mine]),
         (wk_in, gk.at[mine, 0:256]),
         (pos_in.at[0], pos_v),
         (mem_in.at[0], state),
@@ -195,6 +192,11 @@
     from_down, from_up, from_partner = {}, {}, {}
     Q, O, V, K = range(4)
     bufs = (gq, go, gv, gk)
+    order = (
+        (Q, 0), (O, 0), (V, 0), (Q, 1), (O, 1), (K, 0), (Q, 2), (O, 2), (V, 1), (Q, 3), (O, 3), (K, 1),
+        (V, 2, 0), (V, 2, 1), (K, 2, 0), (K, 2, 1), (V, 3), (K, 3),
+    )
+    leave = {0: 3, 1: 4, 2: 5, 3: 6, 4: 7, 5: 8, 6: 9, 7: 10, 8: 11, 9: 12, 10: 13, 11: 14, 12: 15, 13: 16, 14: 17}
 
     def block(d):
         return nz(d) * 2 + c
@@ -203,43 +205,44 @@
         for d in distances:
             from_partner[m, d] = same(bufs[m].at[block(d)], partner)
 
-    def send_own(m):
-        from_down[m] = same(bufs[m].at[block(0)], up)
-        from_up[m] = same(bufs[m].at[block(0)], down)
-
-    def relay(m, d):
-        arrived(from_down[m], bufs[m].at[block(-d)])
-        from_down[m] = same(bufs[m].at[block(-d)], up)
-        arrived(from_up[m], bufs[m].at[block(d)])
-        from_up[m] = same(bufs[m].at[block(d)], down)
-
-    def relay_half(m):
+    def pieces(m, s, later=None):
         rest = slice(128, bufs[m].shape[1])
-        arrived(from_down[m], bufs[m].at[block(-3)])
-        from_down[m] = same(bufs[m].at[block(-3), top], up)
-        arrived(from_up[m], bufs[m].at[block(3)])
-        from_up[m] = same(bufs[m].at[block(3), rest], down)
-
-    def far(m):
-        rest = slice(128, bufs[m].shape[1])
-        arrived(from_down[m], bufs[m].at[block(4), top])
-        arrived(from_up[m], bufs[m].at[block(4), rest])
-        give(m, 4)
+        if s < 3 and later is None:
+            return slice(None), slice(None)
+        return (rest, top) if later else (top, rest)
+
+    def issue(i):
+        m, s = order[i][:2]
+        ahead, behind = pieces(*order[i])
+        from_down[i] = same(bufs[m].at[block(-s), ahead], up)
+        from_up[i] = same(bufs[m].at[block(s), behind], down)
+
+    def ring(*indices):
+        for i in indices:
+            m, s, *later = order[i]
+            ahead, behind = pieces(*order[i])
+            arrived(from_down[i], bufs[m].at[block(-s - 1), ahead])
+            arrived(from_up[i], bufs[m].at[block(s + 1), behind])
+            if i in leave:
+                issue(leave[i])
+            if s == 3:
+                give(m, 4)
+            elif later != [0]:
+                give(m, -s - 1, s + 1)
 
     def take(m, *distances):
         for d in distances:
             arrived(from_partner[m, d], bufs[m].at[nz(d) * 2 + (1 - c)])
 
-    fetched[1].wait()
-    send_own(Q)
-    fetched[2].wait()
-    send_own(O)
-    give(Q, 0)
-    give(O, 0)
-    for copy in fetched[3:]:
+    for i in range(3):
+        fetched[1 + i].wait()
+        issue(i)
+    for copy in fetched[4:]:
         copy.wait()
     rows = jnp.concatenate([wb_v[...].astype(F32), jnp.zeros((14, 256), F32)], axis=0)
     gk[mine, 256:272, :] = rows.astype(BF16)
+    for m in (Q, O, V, K):
+        give(m, 0)
     acc_q[...] = jnp.zeros_like(acc_q)
     acc_k[...] = jnp.zeros_like(acc_k)
     acc_v[...] = jnp.zeros_like(acc_v)
@@ -256,7 +259,6 @@
     f2 = same(xg.at[ny(-1), x, b0], yp)
     arrived(s[3], xg.at[ny(1), x, low])
     f3 = same(xg.at[ny(1), x, b1], yd)
-    relay(Q, 1)
     arrived(f0, xg.at[y, nx(2), a0])
     arrived(f1, xg.at[y, nx(2), a1])
     rows_a = lambda yy, r: xg.at[yy, :, r]
@@ -267,11 +269,7 @@
     rows_b = lambda xx, r: xg.at[:, xx, r]
     s2 = same(rows_b(x, low), xp)
     s3 = same(rows_b(x, low), xd)
-    give(Q, -1, 1)
-    relay(O, 1)
-    give(O, -1, 1)
-    relay(Q, 2)
-    give(Q, -2, 2)
+    ring(0, 1, 2)
 
     arrived(s0, rows_a(ny(-1), top))
     f0 = same(rows_a(ny(-1), a0), yp)
@@ -281,14 +279,7 @@
     f2 = same(rows_b(nx(-1), b0), xp)
     arrived(s3, rows_b(nx(1), low))
     f3 = same(rows_b(nx(1), b1), xd)
-    relay(O, 2)
-    send_own(V)
-    send_own(K)
-    give(O, -2, 2)
-    give(V, 0)
-    give(K, 0)
-    relay_half(Q)
-    give(Q, -3, 3)
+    ring(3, 4)
     arrived(f0, rows_a(ny(2), a0))
     arrived(f1, rows_a(ny(2), a1))
     arrived(f2, rows_b(nx(2), b0))
@@ -302,8 +293,7 @@
     with jax.named_scope("squares"):
         total = lax.fori_loop(0, 16, squares, jnp.zeros((256, 128), F32))
         scale = lax.rsqrt(jnp.sum(total, axis=1, keepdims=True) * (1.0 / 4096) + EPS)
-    relay_half(O)
-    give(O, -3, 3)
+    ring(5)
 
     def normalise(i, carry):
         v = xg[i // 4, lax.rem(i, 4)].astype(F32)
@@ -326,15 +316,11 @@
                 extra = slice(256, 272)
                 logits[...] += dot(left[i], gk[i, extra], NT) + dot(left[i + 1], gk[i + 1, extra], NT)
 
-    relay(V, 1)
-    give(V, -1, 1)
+    ring(6)
     with jax.named_scope("project_q"):
-        project(Q, 0, -1, 1, -2, 2, -3, 3)
-    relay(K, 1)
-    give(K, -1, 1)
-    far(Q)
-    far(O)
-    project(Q, 4)
+        project(Q, 0, -1, 1, -2, 2)
+    ring(7, 8, 9, 10)
+    project(Q, -3, 3, 4)
 
     def wide_state(h):
         high, lo = split(state[h])
@@ -355,27 +341,24 @@
     readout = jnp.concatenate([through(queries(0, h), wides[h]) for h in range(2)], axis=1).astype(BF16)
     take(O, 0, -1, 1, -2, 2, -3, 3, 4)
     scatter = [
-        Scatter(net, [r.at[seg] for r in sums], (x, y), (nx, ny), (xp, xd, yp, yd, x2, y2)) for seg in range(2)
+        Scatter(net, [r.at[seg] for r in sums], (nx, ny), (xp, xd, x2, yp, yd, y2)) for seg in range(2)
     ]
     with jax.named_scope("multiply0"):
         scatter[0].start(readout, go)
-    relay(V, 2)
-    give(V, -2, 2)
+        scatter[0].push(False)
     project(V, 0, -1, 1)
+    ring(11, 12)
     scatter[0].hand_on()
-    relay(K, 2)
-    give(K, -2, 2)
+    ring(13)
     project(K, 0, -1, 1)
-    relay_half(V)
-    give(V, -3, 3)
+    ring(14)
+    project(V, -2, 2)
+    ring(15)
+    project(K, -2, 2)
+    ring(16)
     scatter[0].turn()
-    relay_half(K)
-    give(K, -3, 3)
-    project(V, -2, 2)
-    project(K, -2, 2)
-    far(V)
     project(V, -3, 3)
-    far(K)
+    ring(17)
     project(K, -3, 3)
     project(V, 4)
     project(K, 4)
@@ -405,6 +388,7 @@
 
     for h in range(2):
         update(1, h, got[h][128:192])
+    scatter[1].push(True)
     stored = []
     for h in range(2):
         copy = pltpu.make_async_copy(state.at[h], memory_ref.at[0, h], local.at[h])
@@ -429,7 +413,7 @@
             copy.wait()
 
 
-COPIES = 116
+COPIES = 136
 
 
 def body(hidden_in, w_query, w_key, w_value, w_beta, w_out, mem_pos, memory_in):
@@ -450,16 +434,19 @@
         vmem((128, 256), F32),
         vmem((128, 256), F32),
         vmem((128, 16), F32),
-        vmem((2, 4, 4, 128, 256), BF16),
+        vmem((2, 4, 4, 64, 256), BF16),
         vmem((2, 2, 4, 32, 256), BF16),
         vmem((2, 2, 4, 32, 256), BF16),
         vmem((2, 2, 4, 64, 256), BF16),
-        vmem((2, 4, 64, 256), BF16),
         vmem((2, 3, 64, 256), BF16),
+        vmem((2, 64, 256), F32),
+        vmem((2, 3, 64, 256), BF16),
+        vmem((2, 4, 4, 64, 256), BF16),
         vmem((2, 2, 4, 32, 256), BF16),
         vmem((2, 2, 4, 32, 256), BF16),
         vmem((2, 2, 4, 64, 256), BF16),
-        vmem((2, 4, 64, 256), BF16),
+        vmem((2, 3, 64, 256), BF16),
+        vmem((2, 64, 256), F32),
         vmem((2, 3, 64, 256), BF16),
     ]
     return pl.pallas_call(

time: 71.3 us -> 69.2 us (0.971)
  Pallas kernels: 68.3 us -> 66.2 us
    pallas_call x1, Pallas kernels: 68.3 us -> 66.2 us  [body(): pl.pallas_call(kernel, out_shape=(jax.ShapeDtypeStruct(hidden_in.shape, B...]
where the time goes in v4:
time: 69.2 us; the launch traced here: 69.1 us
  Pallas kernels  66.2 us (96%)
  local copies, waits for them, and re-layouts  2.26 us (3%)
    pallas_call x1, Pallas kernels, body(): pl.pallas_call(kernel, out_shape=(jax.ShapeDtypeStruct(hidden_in.shape, B...  66.2 us
    unnamed x4, local copies, waits for them, and re-layouts  2.26 us

profile of v4, /device:TPU:1, one launch (start us, length us, event | category | flops | bytes accessed | tf_op | source)
XLA Modules:
  0.0 69.1 jit_solution(14340777991830887369)
XLA Ops:
  0.6 66.2 %shard_map.95 = (bf16[1,256,256]{2,1,0:T(8,128)(2,1)}, f32[1,2,128,128]{3,2,1,0:T(8,128)}) custom-call(bf16[1,256,256]{2,1,0:T(8,128)(2,1)} %refs_0_.1, bf16[256,256]{1,0:T(8,128)(2,1)} %refs_1_.1, bf16[256,256]{1,0:T(8,128)(2,1)} %refs_2_.1, bf16[256,256]{1,0:T(8,128)(2,1)} %refs_3_.1, bf16[2,256]{1,0:T(2,128)(2,1)} %bitcast.1, bf16[256,256]{1,0:T(8,128)(2,1)} %refs_5_.1, ...), custom_call_target="tpu_custom_call" | custom-call | tf_op jit(solution)/shard_map/pallas_call | solution.py:452
  66.8 0.0 copy-start
  66.8 1.6 %copy.12 = bf16[1,256,256]{2,1,0:T(8,128)(2,1)} copy(bf16[1,256,256]{2,1,0:T(8,128)(2,1)} %get-tuple-element.4) | data formatting | bytes 262144
  68.4 0.0 copy-done
  68.4 0.7 copy.13
Async XLA Ops:
  66.8 1.6 %copy-start = (f32[1,2,128,128]{3,2,1,0:T(8,128)S(1)}, f32[1,2,128,128]{3,2,1,0:T(8,128)}, u32[]{:S(2)}) copy-start(f32[1,2,128,128]{3,2,1,0:T(8,128)} %get-tuple-element.5) | copy-start | bytes 393220

commit v5 on v4

--- a/solution.py
+++ b/solution.py
@@ -129,6 +129,7 @@
                 mixed += end[i].astype(F32)
             rows = slice(start + j * 64, start + j * 64 + 64)
             out[rows] = (residual[rows].astype(F32) + mixed).astype(BF16)
+            yield rows
 
 
 def split(v):
@@ -144,8 +145,8 @@
 def layer(
     x_in, wq_in, wk_in, wv_in, wb_in, wo_in, pos_in, mem_in,
     out_ref, memory_ref,
-    xg, xn, xm, gv, gq, gk, go, wb_v, pos_v, state, out_v,
-    acc_q, acc_k, acc_v, logits, *rest,
+    xg, xn, xm, gv, gq, gk, go, gb, pos_v, state, out_v,
+    acc_q, acc_k, acc_v, base, logits, *rest,
 ):
     sums, (local, send, recv) = rest[:-3], rest[-3:]
     y, x, z, c = (lax.axis_index(n) for n in ("y", "x", "z", "c"))
@@ -167,9 +168,9 @@
         (x_in.at[0], xg.at[y, x]),
         (wq_in, gq.at[mine]),
         (wo_in, go.at[mine]),
+        (wb_in, gb.at[mine]),
+        (wk_in, gk.at[mine]),
         (wv_in, gv.at[mine]),
-        (wb_in, wb_v),
-        (wk_in, gk.at[mine, 0:256]),
         (pos_in.at[0], pos_v),
         (mem_in.at[0], state),
     ]
@@ -190,11 +191,11 @@
     s = [same(own_a, xp), same(own_a, xd), same(own_b, yp), same(own_b, yd)]
 
     from_down, from_up, from_partner = {}, {}, {}
-    Q, O, V, K = range(4)
-    bufs = (gq, go, gv, gk)
+    Q, O, V, K, B = range(5)
+    bufs = (gq, go, gv, gk, gb)
     order = (
-        (Q, 0), (O, 0), (V, 0), (Q, 1), (O, 1), (K, 0), (Q, 2), (O, 2), (V, 1), (Q, 3), (O, 3), (K, 1),
-        (V, 2, 0), (V, 2, 1), (K, 2, 0), (K, 2, 1), (V, 3), (K, 3),
+        (Q, 0), (O, 0), (K, 0), (Q, 1), (O, 1), (V, 0), (Q, 2), (O, 2), (K, 1), (Q, 3), (O, 3), (V, 1),
+        (K, 2, 0), (K, 2, 1), (V, 2, 0), (V, 2, 1), (K, 3), (V, 3),
     )
     leave = {0: 3, 1: 4, 2: 5, 3: 6, 4: 7, 5: 8, 6: 9, 7: 10, 8: 11, 9: 12, 10: 13, 11: 14, 12: 15, 13: 16, 14: 17}
 
@@ -206,16 +207,19 @@
             from_partner[m, d] = same(bufs[m].at[block(d)], partner)
 
     def pieces(m, s, later=None):
-        rest = slice(128, bufs[m].shape[1])
         if s < 3 and later is None:
             return slice(None), slice(None)
-        return (rest, top) if later else (top, rest)
+        return (low, top) if later else (top, low)
 
     def issue(i):
         m, s = order[i][:2]
         ahead, behind = pieces(*order[i])
         from_down[i] = same(bufs[m].at[block(-s), ahead], up)
         from_up[i] = same(bufs[m].at[block(s), behind], down)
+        if m == K and order[i][2:] != (1,):
+            from_down[B, s] = same(gb.at[block(-s)], up)
+            if s < 3:
+                from_up[B, s] = same(gb.at[block(s)], down)
 
     def ring(*indices):
         for i in indices:
@@ -223,8 +227,14 @@
             ahead, behind = pieces(*order[i])
             arrived(from_down[i], bufs[m].at[block(-s - 1), ahead])
             arrived(from_up[i], bufs[m].at[block(s + 1), behind])
+            if m == K and later != [1]:
+                arrived(from_down[B, s], gb.at[block(-s - 1)])
+                if s < 3:
+                    arrived(from_up[B, s], gb.at[block(s + 1)])
             if i in leave:
                 issue(leave[i])
+            if m == K and later != [1]:
+                give(B, *((-s - 1, s + 1) if s < 3 else (4,)))
             if s == 3:
                 give(m, 4)
             elif later != [0]:
@@ -234,14 +244,13 @@
         for d in distances:
             arrived(from_partner[m, d], bufs[m].at[nz(d) * 2 + (1 - c)])
 
-    for i in range(3):
-        fetched[1 + i].wait()
+    for i, needs in enumerate(((1,), (2,), (3, 4))):
+        for j in needs:
+            fetched[j].wait()
         issue(i)
-    for copy in fetched[4:]:
+    for copy in fetched[5:]:
         copy.wait()
-    rows = jnp.concatenate([wb_v[...].astype(F32), jnp.zeros((14, 256), F32)], axis=0)
-    gk[mine, 256:272, :] = rows.astype(BF16)
-    for m in (Q, O, V, K):
+    for m in (Q, O, V, K, B):
         give(m, 0)
     acc_q[...] = jnp.zeros_like(acc_q)
     acc_k[...] = jnp.zeros_like(acc_k)
@@ -307,14 +316,15 @@
 
     def project(m, *distances):
         take(m, *distances)
+        if m == K:
+            take(B, *distances)
         acc = {Q: acc_q, V: acc_v, K: acc_k}[m]
         left = xn if m == Q else xm
         for d in distances:
             i = nz(d) * 2
-            acc[...] += dot(left[i], bufs[m][i, 0:256]) + dot(left[i + 1], bufs[m][i + 1, 0:256])
+            acc[...] += dot(left[i], bufs[m][i]) + dot(left[i + 1], bufs[m][i + 1])
             if m == K:
-                extra = slice(256, 272)
-                logits[...] += dot(left[i], gk[i, extra], NT) + dot(left[i + 1], gk[i + 1, extra], NT)
+                logits[...] += dot(left[i], gb[i], NT) + dot(left[i + 1], gb[i + 1], NT)
 
     ring(6)
     with jax.named_scope("project_q"):
@@ -338,6 +348,8 @@
         return acc_q[seg_rows[seg], cols[h]] * (128.0 ** -0.5)
 
     wides = [wide_state(h) for h in range(2)]
+    for h in range(2):
+        base[:, cols[h]] = through(queries(1, h), wides[h])
     readout = jnp.concatenate([through(queries(0, h), wides[h]) for h in range(2)], axis=1).astype(BF16)
     take(O, 0, -1, 1, -2, 2, -3, 3, 4)
     scatter = [
@@ -346,48 +358,58 @@
     with jax.named_scope("multiply0"):
         scatter[0].start(readout, go)
         scatter[0].push(False)
-    project(V, 0, -1, 1)
+    project(K, 0, -1, 1)
     ring(11, 12)
     scatter[0].hand_on()
     ring(13)
-    project(K, 0, -1, 1)
+    project(V, 0, -1, 1)
     ring(14)
+    project(K, -2, 2)
+    ring(15)
     project(V, -2, 2)
-    ring(15)
-    project(K, -2, 2)
     ring(16)
+    project(K, -3, 3)
     scatter[0].turn()
     project(V, -3, 3)
+    project(K, 4)
+
+    keys, betas, recalls, matches = [], [], [], []
+    with jax.named_scope("prepare"):
+        for h in range(2):
+            k = acc_k[:, cols[h]]
+            k = k * lax.rsqrt(jnp.sum(k * k, axis=1, keepdims=True) + 1e-06)
+            keys.append(k)
+            betas.append(jax.nn.sigmoid(logits[:, h:h + 1]))
+            kh, kl = split(k[seg_mem[0]])
+            match_high, match_low = split(through(queries(1, h), jnp.concatenate([kh, kl, kh], axis=1)))
+            matches.append(jnp.concatenate([match_high, match_high, match_low], axis=1))
+            recalls.append(through(k[seg_mem[0]], wide_state(h)))
     ring(17)
-    project(K, -3, 3)
     project(V, 4)
-    project(K, 4)
-
-    keys, values, betas = [], [], []
-    for h in range(2):
-        k = acc_k[:, cols[h]]
-        keys.append(k * lax.rsqrt(jnp.sum(k * k, axis=1, keepdims=True) + 1e-06))
-        values.append(acc_v[:, cols[h]])
-        betas.append(jax.nn.sigmoid(logits[:, h:h + 1]))
-
-    def update(seg, h, recalled):
+    values = [acc_v[:, cols[h]] for h in range(2)]
+
+    def change(seg, h, recalled):
         m = seg_mem[seg]
-        ch, cl = split(betas[h][m] * (values[h][m] - recalled))
-        kh, kl = split(keys[h][m])
+        return split(betas[h][m] * (values[h][m] - recalled))
+
+    def update(seg, h, changed):
+        ch, cl = changed
+        kh, kl = split(keys[h][seg_mem[seg]])
         state[h] += dot(jnp.concatenate([ch, ch, cl], axis=0), jnp.concatenate([kh, kl, kh], axis=0), TN)
 
     with jax.named_scope("recur"):
+        changes, readouts = [], []
         for h in range(2):
-            update(0, h, through(keys[h][seg_mem[0]], wide_state(h)))
-        got = []
-        for h in range(2):
-            got.append(through(jnp.concatenate([queries(1, h), keys[h][seg_mem[1]]], axis=0), wide_state(h)))
-        readout = jnp.concatenate([g[0:128] for g in got], axis=1).astype(BF16)
+            ch, cl = change(0, h, recalls[h])
+            changes.append((ch, cl))
+            readouts.append(base[:, cols[h]] + dot(matches[h], jnp.concatenate([ch, cl, ch], axis=0)))
+        readout = jnp.concatenate(readouts, axis=1).astype(BF16)
     with jax.named_scope("multiply1"):
         scatter[1].start(readout, go)
 
     for h in range(2):
-        update(1, h, got[h][128:192])
+        update(0, h, changes[h])
+        update(1, h, change(1, h, through(keys[h][seg_mem[1]], wide_state(h))))
     scatter[1].push(True)
     stored = []
     for h in range(2):
@@ -396,24 +418,23 @@
         stored.append(copy)
 
     def put_out(seg):
-        scatter[seg].last(xg.at[y, x], out_v, seg * 128)
-        part = seg_rows[seg]
-        copy = pltpu.make_async_copy(out_v.at[part], out_ref.at[0, part], local.at[2 + seg])
-        copy.start()
-        stored.append(copy)
+        for part in scatter[seg].last(xg.at[y, x], out_v, seg * 128):
+            copy = pltpu.make_async_copy(out_v.at[part], out_ref.at[0, part], local.at[len(stored)])
+            copy.start()
+            stored.append(copy)
 
     scatter[1].hand_on()
     put_out(0)
     scatter[1].turn()
-    put_out(1)
     with jax.named_scope("drain"):
         net.drain()
+    put_out(1)
     with jax.named_scope("stored"):
         for copy in stored:
             copy.wait()
 
 
-COPIES = 136
+COPIES = 151
 
 
 def body(hidden_in, w_query, w_key, w_value, w_beta, w_out, mem_pos, memory_in):
@@ -424,16 +445,17 @@
         vmem((16, 128, 256), BF16),
         vmem((16, 256, 256), BF16),
         vmem((16, 256, 256), BF16),
-        vmem((16, 272, 256), BF16),
         vmem((16, 256, 256), BF16),
-        vmem((2, 256), BF16),
+        vmem((16, 256, 256), BF16),
+        vmem((16, 2, 256), BF16),
         vmem((2, 64), jnp.int32),
         vmem((2, 128, 128), F32),
         vmem((256, 256), BF16),
         vmem((256, 256), F32),
         vmem((128, 256), F32),
         vmem((128, 256), F32),
-        vmem((128, 16), F32),
+        vmem((128, 256), F32),
+        vmem((128, 2), F32),
         vmem((2, 4, 4, 64, 256), BF16),
         vmem((2, 2, 4, 32, 256), BF16),
         vmem((2, 2, 4, 32, 256), BF16),

time: 69.2 us -> 67.7 us (0.978)
  Pallas kernels: 66.2 us -> 64.6 us
    pallas_call x1, Pallas kernels: 66.2 us -> 64.6 us  [body(): pl.pallas_call(kernel, out_shape=(jax.ShapeDtypeStruct(hidden_in.shape, B...]
where the time goes in v5:
time: 67.7 us; the launch traced here: 67.5 us
  Pallas kernels  64.6 us (95%)
  local copies, waits for them, and re-layouts  2.26 us (3%)
    pallas_call x1, Pallas kernels, body(): pl.pallas_call(kernel, out_shape=(jax.ShapeDtypeStruct(hidden_in.shape, B...  64.6 us
    unnamed x4, local copies, waits for them, and re-layouts  2.26 us

profile of v5, /device:TPU:1, one launch (start us, length us, event | category | flops | bytes accessed | tf_op | source)
XLA Modules:
  0.0 67.5 jit_solution(12627834337681924061)
XLA Ops:
  0.6 64.6 %shard_map.95 = (bf16[1,256,256]{2,1,0:T(8,128)(2,1)}, f32[1,2,128,128]{3,2,1,0:T(8,128)}) custom-call(bf16[1,256,256]{2,1,0:T(8,128)(2,1)} %refs_0_.1, bf16[256,256]{1,0:T(8,128)(2,1)} %refs_1_.1, bf16[256,256]{1,0:T(8,128)(2,1)} %refs_2_.1, bf16[256,256]{1,0:T(8,128)(2,1)} %refs_3_.1, bf16[2,256]{1,0:T(2,128)(2,1)} %bitcast.1, bf16[256,256]{1,0:T(8,128)(2,1)} %refs_5_.1, ...), custom_call_target="tpu_custom_call" | custom-call | tf_op jit(solution)/shard_map/pallas_call | solution.py:474
  65.2 0.0 copy-start
  65.2 1.6 %copy.12 = bf16[1,256,256]{2,1,0:T(8,128)(2,1)} copy(bf16[1,256,256]{2,1,0:T(8,128)(2,1)} %get-tuple-element.4) | data formatting | bytes 262144
  66.8 0.0 copy-done
  66.8 0.7 copy.13
Async XLA Ops:
  65.2 1.6 %copy-start = (f32[1,2,128,128]{3,2,1,0:T(8,128)S(1)}, f32[1,2,128,128]{3,2,1,0:T(8,128)}, u32[]{:S(2)}) copy-start(f32[1,2,128,128]{3,2,1,0:T(8,128)} %get-tuple-element.5) | copy-start | bytes 393220

commit v6 on v5

--- a/solution.py
+++ b/solution.py
@@ -435,6 +435,26 @@
 
 
 COPIES = 151
+
+
+def finish(hidden_in, memory_in, hidden_out, memory_out, hidden, memory):
+    def run(arrive, leave):
+        moves = []
+        for i in range(2):
+            rows = slice(128 * i, 128 * i + 128)
+            moves.append((hidden_in.at[0, rows], hidden.at[rows], hidden_out.at[0, rows]))
+            moves.append((memory_in.at[0, i], memory.at[i], memory_out.at[0, i]))
+        first = [pltpu.make_async_copy(src, via, arrive.at[i]) for i, (src, via, _) in enumerate(moves)]
+        second = [pltpu.make_async_copy(via, dst, leave.at[i]) for i, (_, via, dst) in enumerate(moves)]
+        for copy in first:
+            copy.start()
+        for before, after in zip(first, second):
+            before.wait()
+            after.start()
+        for copy in second:
+            copy.wait()
+
+    pl.run_scoped(run, pltpu.SemaphoreType.DMA((4,)), pltpu.SemaphoreType.DMA((4,)))
 
 
 def body(hidden_in, w_query, w_key, w_value, w_beta, w_out, mem_pos, memory_in):
@@ -471,7 +491,7 @@
         vmem((2, 64, 256), F32),
         vmem((2, 3, 64, 256), BF16),
     ]
-    return pl.pallas_call(
+    results = pl.pallas_call(
         kernel,
         out_shape=(
             jax.ShapeDtypeStruct(hidden_in.shape, BF16),
@@ -484,6 +504,13 @@
             collective_id=0, has_side_effects=True
         ),
     )(hidden_in, w_query, w_key, w_value, w_beta.T, w_out, mem_pos, memory_in)
+    return pl.pallas_call(
+        finish,
+        out_shape=[jax.ShapeDtypeStruct(r.shape, r.dtype) for r in results],
+        in_specs=[pl.BlockSpec(memory_space=pltpu.HBM)] * 2,
+        out_specs=[pl.BlockSpec(memory_space=pltpu.HBM)] * 2,
+        scratch_shapes=[vmem((256, 256), BF16), vmem((2, 128, 128), F32)],
+    )(*results)
 
 
 def solution(mesh):

time: 67.7 us -> 67.1 us (level)
  local copies, waits for them, and re-layouts: 2.26 us -> 0 us
  Pallas kernels: 64.6 us -> 66.1 us
    unnamed x4 -> x0, local copies, waits for them, and re-layouts: 2.26 us -> none
    pallas_call x0 -> x1, Pallas kernels: none -> 1.56 us  [body(): pl.pallas_call(finish, out_shape=[jax.ShapeDtypeStruct(r.shape, r.dtype)...]
where the time goes in v6:
time: 67.1 us; the launch traced here: 66.8 us
  Pallas kernels  66.1 us (99%)
    pallas_call x1, Pallas kernels, body(): pl.pallas_call(kernel, out_shape=(jax.ShapeDtypeStruct(hidden_in.shape, B...  64.6 us
    pallas_call x1, Pallas kernels, body(): pl.pallas_call(finish, out_shape=[jax.ShapeDtypeStruct(r.shape, r.dtype)...  1.56 us

profile of v6, /device:TPU:1, one launch (start us, length us, event | category | flops | bytes accessed | tf_op | source)
XLA Modules:
  0.0 66.8 jit_solution(17948576482779910542)
XLA Ops:
  0.6 64.6 %shard_map.95 = (bf16[1,256,256]{2,1,0:T(8,128)(2,1)}, f32[1,2,128,128]{3,2,1,0:T(8,128)}) custom-call(bf16[1,256,256]{2,1,0:T(8,128)(2,1)} %refs_0_.1, bf16[256,256]{1,0:T(8,128)(2,1)} %refs_1_.1, bf16[256,256]{1,0:T(8,128)(2,1)} %refs_2_.1, bf16[256,256]{1,0:T(8,128)(2,1)} %refs_3_.1, bf16[2,256]{1,0:T(2,128)(2,1)} %bitcast.1, bf16[256,256]{1,0:T(8,128)(2,1)} %refs_5_.1, ...), custom_call_target="tpu_custom_call" | custom-call | tf_op jit(solution)/shard_map/pallas_call | solution.py:494
  65.2 1.6 %shard_map.96 = (bf16[1,256,256]{2,1,0:T(8,128)(2,1)}, f32[1,2,128,128]{3,2,1,0:T(8,128)}) custom-call(bf16[1,256,256]{2,1,0:T(8,128)(2,1)} %get-tuple-element.4.hidden_in, f32[1,2,128,128]{3,2,1,0:T(8,128)} %get-tuple-element.5.memory_in), custom_call_target="tpu_custom_call" | custom-call | tf_op jit(solution)/shard_map/pallas_call | solution.py:507

commit v7 on v6

--- a/solution.py
+++ b/solution.py
@@ -187,8 +187,6 @@
 
     a0, a1, b0, b1 = slice(0, 64), slice(64, 128), slice(128, 192), slice(192, 256)
     top, low = slice(0, 128), slice(128, 256)
-    own_a, own_b = xg.at[y, x, top], xg.at[y, x, low]
-    s = [same(own_a, xp), same(own_a, xd), same(own_b, yp), same(own_b, yd)]
 
     from_down, from_up, from_partner = {}, {}, {}
     Q, O, V, K, B = range(5)
@@ -244,14 +242,15 @@
         for d in distances:
             arrived(from_partner[m, d], bufs[m].at[nz(d) * 2 + (1 - c)])
 
+    own_a, own_b = xg.at[y, x, top], xg.at[y, x, low]
     for i, needs in enumerate(((1,), (2,), (3, 4))):
         for j in needs:
             fetched[j].wait()
         issue(i)
+        if i == 0:
+            s = [same(own_a, xp), same(own_a, xd), same(own_b, yp), same(own_b, yd)]
     for copy in fetched[5:]:
         copy.wait()
-    for m in (Q, O, V, K, B):
-        give(m, 0)
     acc_q[...] = jnp.zeros_like(acc_q)
     acc_k[...] = jnp.zeros_like(acc_k)
     acc_v[...] = jnp.zeros_like(acc_v)
@@ -289,6 +288,8 @@
     arrived(s3, rows_b(nx(1), low))
     f3 = same(rows_b(nx(1), b1), xd)
     ring(3, 4)
+    for m in (Q, O, V, K, B):
+        give(m, 0)
     arrived(f0, rows_a(ny(2), a0))
     arrived(f1, rows_a(ny(2), a1))
     arrived(f2, rows_b(nx(2), b0))
@@ -409,8 +410,9 @@
 
     for h in range(2):
         update(0, h, changes[h])
+    scatter[1].push(True)
+    for h in range(2):
         update(1, h, change(1, h, through(keys[h][seg_mem[1]], wide_state(h))))
-    scatter[1].push(True)
     stored = []
     for h in range(2):
         copy = pltpu.make_async_copy(state.at[h], memory_ref.at[0, h], local.at[h])

time: 67.1 us -> 67.1 us (level)
  no operation moved by 1% of the time
where the time goes in v7:
time: 67.1 us; the launch traced here: 66.8 us
  Pallas kernels  66.1 us (99%)
    pallas_call x1, Pallas kernels, body(): pl.pallas_call(kernel, out_shape=(jax.ShapeDtypeStruct(hidden_in.shape, B...  64.6 us
    pallas_call x1, Pallas kernels, body(): pl.pallas_call(finish, out_shape=[jax.ShapeDtypeStruct(r.shape, r.dtype)...  1.56 us

profile of v7, /device:TPU:1, one launch (start us, length us, event | category | flops | bytes accessed | tf_op | source)
XLA Modules:
  0.0 66.8 jit_solution(14548478302224874943)
XLA Ops:
  0.6 64.6 %shard_map.95 = (bf16[1,256,256]{2,1,0:T(8,128)(2,1)}, f32[1,2,128,128]{3,2,1,0:T(8,128)}) custom-call(bf16[1,256,256]{2,1,0:T(8,128)(2,1)} %refs_0_.1, bf16[256,256]{1,0:T(8,128)(2,1)} %refs_1_.1, bf16[256,256]{1,0:T(8,128)(2,1)} %refs_2_.1, bf16[256,256]{1,0:T(8,128)(2,1)} %refs_3_.1, bf16[2,256]{1,0:T(2,128)(2,1)} %bitcast.1, bf16[256,256]{1,0:T(8,128)(2,1)} %refs_5_.1, ...), custom_call_target="tpu_custom_call" | custom-call | tf_op jit(solution)/shard_map/pallas_call | solution.py:496
  65.2 1.6 %shard_map.96 = (bf16[1,256,256]{2,1,0:T(8,128)(2,1)}, f32[1,2,128,128]{3,2,1,0:T(8,128)}) custom-call(bf16[1,256,256]{2,1,0:T(8,128)(2,1)} %get-tuple-element.4.hidden_in, f32[1,2,128,128]{3,2,1,0:T(8,128)} %get-tuple-element.5.memory_in), custom_call_target="tpu_custom_call" | custom-call | tf_op jit(solution)/shard_map/pallas_call | solution.py:509

commit v8 on v7

--- a/solution.py
+++ b/solution.py
@@ -79,18 +79,21 @@
         for (p, half, *_), to, _ in self.sides:
             for i in range(2):
                 self.h.append(self.net.post(p.at[2, :, 32 * i:32 * i + 32], half.at[i], to[i]))
+        self.f = []
+        self.near(slice(0, 1))
         self.multiply(rows, weights, 1)
         self.multiply(rows, weights, 0)
+
+    def near(self, part):
+        for (p, _, _, full, *_), to, _ in self.sides:
+            for i in range(2):
+                self.f.append(self.net.post(p.at[1 + 2 * i, part], full.at[i, part], to[i]))
 
     def push(self, wait):
         if wait:
             for slot in self.h:
                 self.net.gone(slot)
-        self.f = []
-        for part in (slice(0, 1), slice(1, 4)):
-            for (p, _, _, full, *_), to, _ in self.sides:
-                for i in range(2):
-                    self.f.append(self.net.post(p.at[1 + 2 * i, part], full.at[i, part], to[i]))
+        self.near(slice(1, 4))
 
     def hand_on(self):
         early, late = [], []

time: 67.1 us -> 67.2 us (level)
  no operation moved by 1% of the time
where the time goes in v8:
time: 67.2 us; the launch traced here: 66.8 us
  Pallas kernels  66.1 us (98%)
    pallas_call x1, Pallas kernels, body(): pl.pallas_call(kernel, out_shape=(jax.ShapeDtypeStruct(hidden_in.shape, B...  64.6 us
    pallas_call x1, Pallas kernels, body(): pl.pallas_call(finish, out_shape=[jax.ShapeDtypeStruct(r.shape, r.dtype)...  1.56 us

profile of v8, /device:TPU:1, one launch (start us, length us, event | category | flops | bytes accessed | tf_op | source)
XLA Modules:
  0.0 66.8 jit_solution(8023318260766747753)
XLA Ops:
  0.6 64.6 %shard_map.95 = (bf16[1,256,256]{2,1,0:T(8,128)(2,1)}, f32[1,2,128,128]{3,2,1,0:T(8,128)}) custom-call(bf16[1,256,256]{2,1,0:T(8,128)(2,1)} %refs_0_.1, bf16[256,256]{1,0:T(8,128)(2,1)} %refs_1_.1, bf16[256,256]{1,0:T(8,128)(2,1)} %refs_2_.1, bf16[256,256]{1,0:T(8,128)(2,1)} %refs_3_.1, bf16[2,256]{1,0:T(2,128)(2,1)} %bitcast.1, bf16[256,256]{1,0:T(8,128)(2,1)} %refs_5_.1, ...), custom_call_target="tpu_custom_call" | custom-call | tf_op jit(solution)/shard_map/pallas_call | solution.py:499
  65.2 1.6 %shard_map.96 = (bf16[1,256,256]{2,1,0:T(8,128)(2,1)}, f32[1,2,128,128]{3,2,1,0:T(8,128)}) custom-call(bf16[1,256,256]{2,1,0:T(8,128)(2,1)} %get-tuple-element.4.hidden_in, f32[1,2,128,128]{3,2,1,0:T(8,128)} %get-tuple-element.5.memory_in), custom_call_target="tpu_custom_call" | custom-call | tf_op jit(solution)/shard_map/pallas_call | solution.py:512
